TPU v7x, 128 devices: a whole 4x4x4 slice. The times are simulated.
128 devices in a mesh: dp: 4 (over z), row: 4 (over y), fsdp: 8 (over x, core).
Axes of the slice: x: 4, y: 4, z: 4, core: 2. Of those that a mesh axis runs over, the one named last changes fastest.
Arguments:
- x_saved: bfloat16 [2, 262144, 288], P(None, ('dp', 'row', 'fsdp'))
- dy_out: bfloat16 [2, 262144, 288], P(None, ('dp', 'row', 'fsdp'))
- w_gate: bfloat16 [288, 768], P(None, ('row', 'fsdp'))
- w_up: bfloat16 [288, 768], P(None, ('row', 'fsdp'))
- w_down: bfloat16 [768, 288], P(('row', 'fsdp'))
- g_next: float32 [128, 3, 288, 768], P(('dp', 'row', 'fsdp'))
Outputs:
- output 1: bfloat16 [2, 262144, 288], P(None, ('dp', 'row', 'fsdp'))
- output 2: float32 [3, 288, 768], P(None, None, ('row', 'fsdp'))
- output 3: float32 [128, 3, 288, 768], P(('dp', 'row', 'fsdp'))
All inputs are finite; a program needn't handle non-finite values.
Results may differ from a plain program's by a relative error of at most 0.0145274.
Values are sent between devices in bfloat16 or wider.
A program may use at most 1 GiB of HBM per device.

v0:
```python
import jax
import jax.numpy as jnp
from jax import lax
from jax.sharding import PartitionSpec as P

TOK_AXES = ("dp", "row", "fsdp")
GROUP_AXES = ("row", "fsdp")


def mlp_backward(x_flat, dy_flat, w_gate, w_up, w_down):
    pre_gate = jnp.dot(x_flat, w_gate, preferred_element_type=jnp.float32)
    pre_up = jnp.dot(x_flat, w_up, preferred_element_type=jnp.float32)
    sig_gate = jax.nn.sigmoid(pre_gate)
    act_gate = pre_gate * sig_gate
    hidden = (act_gate * pre_up).astype(jnp.bfloat16)
    d_hidden = jnp.einsum("td,fd->tf", dy_flat, w_down, preferred_element_type=jnp.float32)
    d_gate = (d_hidden * pre_up * sig_gate * (1.0 + pre_gate * (1.0 - sig_gate))).astype(jnp.bfloat16)
    d_up = (d_hidden * act_gate).astype(jnp.bfloat16)
    dx_flat = (jnp.einsum("tf,df->td", d_gate, w_gate, preferred_element_type=jnp.float32) + jnp.einsum("tf,df->td", d_up, w_up, preferred_element_type=jnp.float32)).astype(jnp.bfloat16)
    grad_layer = jnp.stack([
        jnp.einsum("td,tf->df", x_flat, d_gate, preferred_element_type=jnp.float32),
        jnp.einsum("td,tf->df", x_flat, d_up, preferred_element_type=jnp.float32),
        jnp.einsum("td,tf->df", dy_flat, hidden, preferred_element_type=jnp.float32),
    ])
    return dx_flat, grad_layer


def solution(mesh):
    def local_step(x_dev, dy_dev, gate_shard, up_shard, down_shard, g_dev):
        w_gate = lax.all_gather(gate_shard, GROUP_AXES, axis=1, tiled=True)
        w_up = lax.all_gather(up_shard, GROUP_AXES, axis=1, tiled=True)
        w_down = lax.all_gather(down_shard, GROUP_AXES, axis=0, tiled=True)
        g_shard = lax.psum_scatter(g_dev[0].astype(jnp.bfloat16), GROUP_AXES, scatter_dimension=2, tiled=True)
        grad_next = lax.psum(g_shard.astype(jnp.float32), "dp")
        micro_count, tok_dev, d_model = x_dev.shape
        dx_flat, grad_layer = mlp_backward(x_dev.reshape(micro_count * tok_dev, d_model), dy_dev.reshape(micro_count * tok_dev, d_model), w_gate, w_up, w_down)
        return dx_flat.reshape(micro_count, tok_dev, d_model), grad_next, grad_layer[None]

    in_specs = (P(None, TOK_AXES, None), P(None, TOK_AXES, None), P(None, GROUP_AXES), P(None, GROUP_AXES), P(GROUP_AXES, None), P(TOK_AXES, None, None, None))
    out_specs = (P(None, TOK_AXES, None), P(None, None, GROUP_AXES), P(TOK_AXES, None, None, None))
    return jax.shard_map(local_step, mesh=mesh, in_specs=in_specs, out_specs=out_specs, check_vma=False)
```

profile of v0, /device:TPU:1, one launch (start us, length us, event | category | flops | bytes accessed | tf_op | source)
XLA Modules:
  0.0 191.1 jit_solution(11929427475726464751)
XLA Ops:
  7.2 0.0 all-reduce.6.cloned.1.call-start
  7.2 3.0 %copy.17 = bf16[1,3,288,768]{2,3,1,0:T(8,128)(2,1)} copy(f32[1,3,288,768]{3,2,1,0:T(8,128)} %param.11) | data formatting | bytes 3981312 | tf_op args[5]
  10.2 0.0 all-reduce.6.cloned.1.call-update
  10.2 0.0 all-reduce.4.cloned.1.call-start
  10.3 26.6 %all_gather.11 = bf16[288,768]{0,1:T(8,128)(2,1)S(1)} all-gather(bf16[288,24]{0,1:T(8,128)(2,1)} %param.8), channel_id=1, replica_groups=mesh['dp'=4,'row'=4,'fsdp'=8] {'row','fsdp'}, dimensions={1}, use_global_device_ids=true | all-gather | bytes 456192 | tf_op jit(solution)/shard_map/all_gather | solution.py:30
  36.9 24.4 %all_gather.10 = bf16[288,768]{0,1:T(8,128)(2,1)S(1)} all-gather(bf16[288,24]{0,1:T(8,128)(2,1)S(1)} %copy-done.5), channel_id=1, replica_groups=mesh['dp'=4,'row'=4,'fsdp'=8] {'row','fsdp'}, dimensions={1}, use_global_device_ids=true | all-gather | bytes 456192 | tf_op jit(solution)/shard_map/all_gather | solution.py:31
  61.2 22.5 %all_gather.9 = bf16[768,288]{1,0:T(8,128)(2,1)S(1)} all-gather(bf16[24,288]{1,0:T(8,128)(2,1)S(1)} %copy-done.6), channel_id=1, replica_groups=mesh['dp'=4,'row'=4,'fsdp'=8] {'row','fsdp'}, dimensions={0}, use_global_device_ids=true | all-gather | bytes 456192 | tf_op jit(solution)/shard_map/all_gather | solution.py:32
  83.7 1.8 copy.23
  85.6 1.6 copy.22
  87.1 3.5 %fusion.7 = f32[4096,768]{1,0:T(8,128)S(1)} fusion(bf16[4096,288]{0,1:T(8,128)(2,1)S(1)} %bitcast.45, bf16[288,768]{0,1:T(8,128)(2,1)S(1)} %all_gather.11), kind=kOutput, calls=%fused_computation.17 | convolution fusion | flops 1811939328 | bytes 15384576 | tf_op jit(solution)/shard_map/dot_general | solution.py:11
  90.6 6.4 %fusion.6 = f32[4096,768]{1,0:T(8,128)} fusion(bf16[4096,288]{0,1:T(8,128)(2,1)S(1)} %bitcast.46, bf16[288,768]{0,1:T(8,128)(2,1)S(1)} %all_gather.10), kind=kOutput, calls=%fused_computation.16 | convolution fusion | flops 1811939328 | bytes 15384576 | tf_op jit(solution)/shard_map/dot_general | solution.py:12
  97.0 2.4 %copy-done.2 = f32[4096,768]{1,0:T(8,128)} copy-done((f32[4096,768]{1,0:T(8,128)}, f32[4096,768]{1,0:T(8,128)S(1)}, u32[]{:S(2)}) %copy-start.2) | copy-done | bytes 12582936
  99.4 7.4 %fusion.4 = f32[1,288,768]{2,1,0:T(8,128)S(1)} fusion(bf16[4096,288]{0,1:T(8,128)(2,1)S(1)} %bitcast.54, f32[4096,768]{1,0:T(8,128)} %fusion.6, f32[4096,768]{1,0:T(8,128)S(1)} %fusion.7), kind=kOutput, calls=%fused_computation.11 | convolution fusion | flops 1830813696 | bytes 28409856 | tf_op jit(solution)/shard_map/td,tf->df/dot_general | solution.py:23
  106.8 16.9 %multiply_convert_fusion.1 = (bf16[4096,768]{1,0:T(8,128)(2,1)}, bf16[4096,768]{1,0:T(8,128)(2,1)}) fusion(f32[4096,768]{1,0:T(8,128)} %copy-done.2, f32[4096,768]{1,0:T(8,128)} %fusion.6, bf16[4096,288]{0,1:T(8,128)(2,1)S(1)} %bitcast.55, bf16[768,288]{1,0:T(8,128)(2,1)S(1)} %all_gather.9), kind=kOutput, calls=%fused_computation.1 | convolution fusion | flops 1852833792 | bytes 40550400 | tf_op jit(solution)/shard_map/td,fd->tf/dot_general | solution.py:16
  123.7 5.1 %fusion.8 = f32[4096,288]{0,1:T(8,128)S(1)} fusion(bf16[4096,768]{1,0:T(8,128)(2,1)} %get-tuple-element.13, bf16[288,768]{0,1:T(8,128)(2,1)S(1)} %all_gather.11), kind=kOutput, calls=%fused_computation.18 | convolution fusion | flops 1811939328 | bytes 11452416 | tf_op jit(solution)/shard_map/tf,df->td/dot_general | solution.py:19
  128.8 3.7 %fusion.2 = bf16[4096,288]{0,1:T(8,128)(2,1)} fusion(f32[4096,288]{0,1:T(8,128)S(1)} %fusion.8, bf16[4096,768]{1,0:T(8,128)(2,1)S(1)} %copy-done, bf16[288,768]{0,1:T(8,128)(2,1)S(1)} %all_gather.10), kind=kOutput, calls=%fused_computation.7 | convolution fusion | flops 1814298624 | bytes 13811712 | tf_op jit(solution)/shard_map/tf,df->td/dot_general | solution.py:19
  132.5 3.0 %convolution_bitcast_fusion = f32[1,288,768]{2,1,0:T(8,128)} fusion(bf16[4096,288]{0,1:T(8,128)(2,1)S(1)} %bitcast.47, bf16[4096,768]{1,0:T(8,128)(2,1)S(1)} %copy-done), kind=kOutput, calls=%fused_computation.12 | convolution fusion | flops 1811939328 | bytes 9535488 | tf_op jit(solution)/shard_map/td,tf->df/dot_general | solution.py:22
  135.5 0.6 dynamic-slice
  136.7 5.7 %convolution_bitcast_fusion.1 = f32[1,288,768]{2,1,0:T(8,128)} fusion(bf16[4096,288]{0,1:T(8,128)(2,1)S(1)} %bitcast.48, bf16[4096,768]{1,0:T(8,128)(2,1)} %get-tuple-element.13), kind=kOutput, calls=%fused_computation.13 | convolution fusion | flops 1811939328 | bytes 9535488 | tf_op jit(solution)/shard_map/td,tf->df/dot_general | solution.py:21
  142.4 1.6 dynamic-slice_convert_fusion
  144.1 3.1 %maximum_bitcast_fusion = f32[1,3,288,768]{3,2,1,0:T(8,128)} fusion(f32[1,288,768]{2,1,0:T(8,128)S(1)} %fusion.4, f32[1,288,768]{2,1,0:T(8,128)} %convolution_bitcast_fusion, f32[1,288,768]{2,1,0:T(8,128)} %convolution_bitcast_fusion.1), kind=kLoop, calls=%fused_computation.8 | loop fusion | flops 1327104 | bytes 5308416 | tf_op jit(solution)/shard_map/broadcast_in_dim | solution.py:37
  147.2 1.6 copy.25
  148.8 34.0 %all-reduce.4.cloned.1.call-done = f32[3,288,24]{1,2,0:T(8,128)} async-done(((f32[3,288,24]{1,2,0:T(8,128)}), f32[3,288,24]{1,2,0:T(8,128)}) %all-reduce.4.cloned.1.call-update) | async-done | bytes 82960 | tf_op jit(solution)/shard_map/psum | solution.py:34
  182.7 1.5 copy.28
  (17 shorter events, 0.1 us)
Async XLA Ops:
  7.2 29.7 %copy-start.5 = (bf16[288,24]{0,1:T(8,128)(2,1)S(1)}, bf16[288,24]{0,1:T(8,128)(2,1)}, u32[]{:S(2)}) copy-start(bf16[288,24]{0,1:T(8,128)(2,1)} %param.9) | copy-start | bytes 41476
  7.2 54.0 %copy-start.6 = (bf16[24,288]{1,0:T(8,128)(2,1)S(1)}, bf16[24,288]{1,0:T(8,128)(2,1)}, u32[]{:S(2)}) copy-start(bf16[24,288]{1,0:T(8,128)(2,1)} %param.10) | copy-start | bytes 41476
  7.2 135.3 %all-reduce.6.cloned.1.call-start = ((), (), s32[]{:S(2)}) async-start(), calls=%async_computation.1 | async-start | bytes 3538944
  10.2 172.5 %all-reduce.4.cloned.1.call-start = ((), (), s32[]{:S(2)}) async-start(), calls=%async_computation | async-start | bytes 221184 | tf_op jit(solution)/shard_map/psum | solution.py:34
  10.3 75.3 %copy-start.3 = (bf16[2,2048,288]{1,2,0:T(8,128)(2,1)S(1)}, bf16[2,2048,288]{1,2,0:T(8,128)(2,1)}, u32[]{:S(2)}) copy-start(bf16[2,2048,288]{1,2,0:T(8,128)(2,1)} %param.7) | copy-start | bytes 7077892
  90.6 8.8 %copy-start.2 = (f32[4096,768]{1,0:T(8,128)}, f32[4096,768]{1,0:T(8,128)S(1)}, u32[]{:S(2)}) copy-start(f32[4096,768]{1,0:T(8,128)S(1)} %fusion.7) | copy-start | bytes 37748740
  90.6 8.8 %copy-start.4 = (bf16[2,36,8,2048]{3,2,0,1:T(8,128)(2,1)S(1)}, bf16[2,36,8,2048]{3,2,0,1:T(8,128)(2,1)}, u32[]{:S(2)}) copy-start(bf16[2,36,8,2048]{3,2,0,1:T(8,128)(2,1)} %copy.22) | copy-start | bytes 7077892
  123.7 5.1 %copy-start = (bf16[4096,768]{1,0:T(8,128)(2,1)S(1)}, bf16[4096,768]{1,0:T(8,128)(2,1)}, u32[]{:S(2)}) copy-start(bf16[4096,768]{1,0:T(8,128)(2,1)} %get-tuple-element.12) | copy-start | bytes 18874372
  132.5 3.0 %copy-start.7 = (u32[128]{0:T(128)S(1)}, u32[128]{0:T(128)}, u32[]{:S(2)}) copy-start(u32[128]{0:T(128)} %constant.8) | copy-start | bytes 1540
  142.4 4.8 %copy-start.1 = (bf16[4096,288]{0,1:T(8,128)(2,1)S(1)}, bf16[4096,288]{0,1:T(8,128)(2,1)}, u32[]{:S(2)}) copy-start(bf16[4096,288]{0,1:T(8,128)(2,1)} %fusion.2) | copy-start | bytes 7077892
Sparse Core Ops, SparseCore 0:
  11.9 110.2 all-reduce.5
  144.2 38.4 all-reduce.3
where the time goes:
time: 193 us; the launch traced here: 191 us
  blocking collectives  73.5 us (38%)
  matrix products  51.6 us (27%)
  waiting for transfers between devices  34 us (18%)
  between operations  14.8 us (8%)
  local copies, waits for them, and re-layouts  12.5 us (6%)
  other arithmetic  4.72 us (2%)
    psum x1, waiting for transfers between devices, local_step(): grad_next = lax.psum(g_shard.astype(jnp.float32), 'dp')  34 us
    all_gather x1, blocking collectives, local_step(): w_gate = lax.all_gather(gate_shard, GROUP_AXES, axis=1, tiled=True)  26.6 us
    all_gather x1, blocking collectives, local_step(): w_up = lax.all_gather(up_shard, GROUP_AXES, axis=1, tiled=True)  24.4 us
    all_gather x1, blocking collectives, local_step(): w_down = lax.all_gather(down_shard, GROUP_AXES, axis=0, tiled=True)  22.5 us
    dot_general x1, matrix products, mlp_backward(): jnp.einsum('td,fd->tf', dy_flat, w_down, preferred_element_type=jnp.float32)  16.9 us
    unnamed x19, local copies, waits for them, and re-layouts  7.54 us
    dot_general x1, matrix products, mlp_backward(): jnp.einsum('td,tf->df', dy_flat, hidden, preferred_element_type=jnp.float32)  7.4 us
    dot_general x1, matrix products, mlp_backward(): pre_up = jnp.dot(x_flat, w_up, preferred_element_type=jnp.float32)  6.36 us
  transfers between devices with their start and end apart: 2, of which 1 were waited for; matrix products, arithmetic and copies ran while one was open for 32% of the time, Pallas kernels for 0%

commit v1 on v0

v1 whole, which is shorter than its diff:
```python
import jax
import jax.numpy as jnp
from jax import lax
from jax.experimental import pallas as pl
from jax.experimental.pallas import tpu as pltpu
from jax.sharding import PartitionSpec as P

TOK_AXES = ("dp", "row", "fsdp")
GROUP_AXES = ("row", "fsdp")
F32, BF16 = jnp.float32, jnp.bfloat16
MESH = pl.DeviceIdType.MESH
TILE = 512
NN = (((1,), (0,)), ((), ()))
NT = (((1,), (1,)), ((), ()))


def mm(lhs, rhs, dims=NN):
    return lax.dot_general(lhs, rhs, dims, preferred_element_type=F32)


def kernel(n_dp, n_row, n_x, micro, tokens, d_model, ff, blk,
           x_hbm, dy_hbm, w1_ref, w3_ref, w2_ref, g_hbm,
           dx_hbm, gn_ref, dw_hbm,
           x_v, dy_v, dx_v, acc, g_v,
           wa, wb, w1t, w3t, w2t, w1, w3,
           gt, pr, part, rx1, up, rx2, q, ry, r, rz,
           load_sem, g_sem, out_sem, ag_s, ag_r, rs_s, rs_r):
    z, y, f = lax.axis_index("dp"), lax.axis_index("row"), lax.axis_index("fsdp")
    x, c = f // 2, f % 2
    main, tail = 256, d_model - 256

    def at_x(d):
        return (z, y, ((x + d) % n_x) * 2 + c)

    def at_y(d):
        return (z, (y + d) % n_row, f)

    def at_z(d):
        return ((z + d) % n_dp, y, f)

    partner = (z, y, x * 2 + 1 - c)
    peers = [partner] + [at_x(d) for d in range(1, n_x)] + [at_y(d) for d in range(1, n_row)]
    peers += [at_z(d) for d in range(1, n_dp)]

    barrier = pltpu.get_barrier_semaphore()
    for peer in peers:
        pl.semaphore_signal(barrier, inc=1, device_id=peer, device_id_type=MESH)

    g_loads = [pltpu.make_async_copy(g_hbm.at[s], g_v.at[s], g_sem.at[s]) for s in range(3)]
    x_load = pltpu.make_async_copy(x_hbm, x_v, load_sem.at[0])
    dy_load = pltpu.make_async_copy(dy_hbm, dy_v, load_sem.at[1])
    for load in g_loads + [x_load, dy_load]:
        load.start()

    s1, s3, s2 = w1_ref[...], w3_ref[...], w2_ref[...]
    wa[y, x, c, :, :main] = s1[:, :main]
    wa[y, x, c, :, main:] = s3[:, :main]
    wb[y, x, c, :, :main] = s2[:, :main]
    tails = [s[:, main:].astype(F32) for s in (s1, s3, s2)] + [jnp.zeros((blk, 128 - 3 * tail), F32)]
    wb[y, x, c, :, main:] = jnp.concatenate(tails, axis=1).astype(BF16)

    pl.semaphore_wait(barrier, len(peers))

    count = {"ag": 0, "rs": 0}

    def send(kind, src, dst, device):
        i = count[kind]
        count[kind] += 1
        ss, rr = (ag_s, ag_r) if kind == "ag" else (rs_s, rs_r)
        copy = pltpu.make_async_remote_copy(
            src_ref=src, dst_ref=dst, send_sem=ss.at[i], recv_sem=rr.at[i],
            device_id=device, device_id_type=MESH)
        copy.start()
        sent.append(copy)
        return copy

    sent = []

    def push(ref, device):
        return send("ag", ref, ref, device)

    a1 = [push(wa.at[y, x, c], at_x(d)) for d in (1, 3, 2)]
    b1 = [push(wb.at[y, x, c], at_y(d)) for d in (1, 3, 2)]

    def turn(s):
        g_loads[s].wait()
        flat = g_v[s, :main, :].T.reshape(n_row, n_x, 2, blk, main)
        gt[..., s * main:(s + 1) * main] = flat.astype(BF16)

    def turn_tail():
        rows = [g_v[s, main:, :] for s in range(3)] + [jnp.zeros((128 - 3 * tail, ff), F32)]
        flat = jnp.concatenate(rows, axis=0).T.reshape(n_row, n_x, 2, blk, 128)
        gt[..., 3 * main:] = flat.astype(BF16)

    turn(0)
    turn(1)

    for copy in a1:
        copy.wait_recv()
    a2 = [push(wa.at[y, :, c], at_y(1)), push(wa.at[y, :, c], at_y(n_row - 1))]
    ad = [push(wa.at[y, :, c], partner)]
    for copy in b1:
        copy.wait_recv()
    b2 = [push(wb.at[:, x, c], at_x(1)), push(wb.at[:, x, c], at_x(n_x - 1))]
    bd = [push(wb.at[:, x, c], partner)]

    turn(2)
    turn_tail()
    pair = send("rs", gt.at[:, :, 1 - c], pr, partner)

    ym, yp, yo = (y + n_row - 1) % n_row, (y + 1) % n_row, (y + 2) % n_row
    xm, xp, xo = (x + n_x - 1) % n_x, (x + 1) % n_x, (x + 2) % n_x
    a2[0].wait_recv()
    a3 = [push(wa.at[ym, pl.ds(0, 2), c], at_y(1))]
    ad.append(push(wa.at[ym, :, c], partner))
    a2[1].wait_recv()
    a3.append(push(wa.at[yp, pl.ds(2, 2), c], at_y(n_row - 1)))
    ad.append(push(wa.at[yp, :, c], partner))
    b2[0].wait_recv()
    b3 = [push(wb.at[pl.ds(0, 2), xm, c], at_x(1))]
    bd.append(push(wb.at[:, xm, c], partner))
    b2[1].wait_recv()
    b3.append(push(wb.at[pl.ds(2, 2), xp, c], at_x(n_x - 1)))
    bd.append(push(wb.at[:, xp, c], partner))

    pair.wait_recv()
    part[...] = (gt[:, :, c].astype(F32) + pr[...].astype(F32)).astype(BF16)
    hy = n_row // 2

    for copy in a3:
        copy.wait_recv()
    ad.append(push(wa.at[yo, :, c], partner))
    for copy in b3:
        copy.wait_recv()
    bd.append(push(wb.at[:, xo, c], partner))

    x1 = [send("rs", part.at[pl.ds(0, hy), xo], rx1.at[0], at_x(1)),
          send("rs", part.at[pl.ds(hy, hy), xo], rx1.at[1], at_x(n_x - 1))]

    acc[...] = jnp.zeros_like(acc)
    for copy in ad + bd:
        copy.wait_recv()

    def flat(ref, lo, hi):
        return ref[..., lo:hi].astype(F32).reshape(ff, hi - lo).astype(BF16)

    m1, m3, m2, mt = flat(wa, 0, main), flat(wa, main, 2 * main), flat(wb, 0, main), flat(wb, main, main + 128)
    w1t[:, :main] = m1
    w3t[:, :main] = m3
    w2t[:, :main] = m2
    w1t[:, main:] = mt[:, :tail]
    w3t[:, main:] = mt[:, tail:2 * tail]
    w2t[:, main:] = mt[:, 2 * tail:3 * tail]
    w1[:main, :] = m1.T
    w3[:main, :] = m3.T
    tail_t = mt.T
    w1[main:, :] = tail_t[:tail]
    w3[main:, :] = tail_t[tail:2 * tail]
    x_load.wait()
    dy_load.wait()

    per = tokens // TILE
    steps = micro * per

    def stage_up():
        for copy in x1:
            copy.wait_recv()
        up[0, hy:] = part[hy:, xp]
        up[0, :hy] = (part[:hy, xp].astype(F32) + rx1[0].astype(F32)).astype(BF16)
        up[1, :hy] = part[:hy, xm]
        up[1, hy:] = (part[hy:, xm].astype(F32) + rx1[1].astype(F32)).astype(BF16)

    def out_copy(i):
        m, t = i // per, i % per
        where = pl.ds(pl.multiple_of(t * TILE, TILE), TILE)
        return pltpu.make_async_copy(dx_v.at[m, :, where], dx_hbm.at[m, :, where], out_sem.at[i])

    def step(i, carry):
        m, t = i // per, i % per
        where = pl.ds(pl.multiple_of(t * TILE, TILE), TILE)
        xt, dyt = x_v[m, :, where], dy_v[m, :, where]
        a, b, dh = mm(w1t[...], xt), mm(w3t[...], xt), mm(w2t[...], dyt)
        sig = 0.5 * jnp.tanh(0.5 * a) + 0.5
        act = a * sig
        h = (act * b).astype(BF16)
        db = (dh * act).astype(BF16)
        da = (dh * b * (sig + act * (1.0 - sig))).astype(BF16)
        dx_v[m, :, where] = (mm(w1[...], da) + mm(w3[...], db)).astype(BF16)
        acc[0] += mm(xt, da, NT)
        acc[1] += mm(xt, db, NT)
        acc[2] += mm(dyt, h, NT)
        out_copy(i).start()
        return carry

    quarter = steps // 4
    lax.fori_loop(0, quarter, step, 0)
    stage_up()
    x2 = [send("rs", up.at[0], rx2.at[0], at_x(1)), send("rs", up.at[1], rx2.at[1], at_x(n_x - 1))]
    lax.fori_loop(quarter, 2 * quarter, step, 0)
    for copy in x2:
        copy.wait_recv()
    q[...] = (part[:, x].astype(F32) + rx2[0].astype(F32) + rx2[1].astype(F32)).astype(BF16)
    ys = [send("rs", q.at[(y + d) % n_row], ry.at[d - 1], at_y(d)) for d in range(1, n_row)]
    lax.fori_loop(2 * quarter, 3 * quarter, step, 0)
    for copy in ys:
        copy.wait_recv()
    own = q[y].astype(F32)
    for d in range(1, n_row):
        own += ry[d - 1].astype(F32)
    r[...] = own.astype(BF16)
    zs = [send("rs", r, rz.at[z], at_z(d)) for d in range(1, n_dp)]
    rz[z] = r[...]
    lax.fori_loop(3 * quarter, steps, step, 0)
    dw_out = [pltpu.make_async_copy(acc.at[s], dw_hbm.at[s], g_sem.at[s]) for s in range(3)]
    for copy in dw_out:
        copy.start()
    for copy in zs:
        copy.wait_recv()
    total = rz[0].astype(F32)
    for d in range(1, n_dp):
        total += rz[d].astype(F32)
    for s in range(3):
        gn_ref[s, :, :main] = total[:, s * main:(s + 1) * main]
        gn_ref[s, :, main:] = total[:, 3 * main + s * tail:3 * main + (s + 1) * tail]
    for copy in sent:
        copy.wait_send()
    for copy in dw_out:
        copy.wait()
    for i in range(steps):
        out_copy(i).wait()


def solution(mesh):
    n_dp, n_row, n_x = mesh.shape["dp"], mesh.shape["row"], mesh.shape["fsdp"] // 2

    def local_step(x_dev, dy_dev, gate, up_w, down, g_dev):
        micro, tokens, d_model = x_dev.shape
        blk = gate.shape[1]
        ff = blk * n_row * n_x * 2
        wide = 3 * 256 + 128
        vmem = pl.BlockSpec(memory_space=pltpu.VMEM)
        hbm = pl.BlockSpec(memory_space=pltpu.HBM)

        def body(*refs):
            kernel(n_dp, n_row, n_x, micro, tokens, d_model, ff, blk, *refs)

        steps = micro * (tokens // TILE)
        dx_t, gn, dw = pl.pallas_call(
            body,
            in_specs=[hbm, hbm, vmem, vmem, vmem, hbm],
            out_specs=[hbm, vmem, hbm],
            out_shape=[
                jax.ShapeDtypeStruct((micro, d_model, tokens), BF16),
                jax.ShapeDtypeStruct((3, blk, d_model), F32),
                jax.ShapeDtypeStruct((3, d_model, ff), F32),
            ],
            scratch_shapes=[
                pltpu.VMEM((micro, d_model, tokens), BF16),
                pltpu.VMEM((micro, d_model, tokens), BF16),
                pltpu.VMEM((micro, d_model, tokens), BF16),
                pltpu.VMEM((3, d_model, ff), F32),
                pltpu.VMEM((3, d_model, ff), F32),
                pltpu.VMEM((n_row, n_x, 2, blk, 512), BF16),
                pltpu.VMEM((n_row, n_x, 2, blk, 384), BF16),
                pltpu.VMEM((ff, d_model), BF16),
                pltpu.VMEM((ff, d_model), BF16),
                pltpu.VMEM((ff, d_model), BF16),
                pltpu.VMEM((d_model, ff), BF16),
                pltpu.VMEM((d_model, ff), BF16),
                pltpu.VMEM((n_row, n_x, 2, blk, wide), BF16),
                pltpu.VMEM((n_row, n_x, blk, wide), BF16),
                pltpu.VMEM((n_row, n_x, blk, wide), BF16),
                pltpu.VMEM((2, n_row // 2, blk, wide), BF16),
                pltpu.VMEM((2, n_row, blk, wide), BF16),
                pltpu.VMEM((2, n_row, blk, wide), BF16),
                pltpu.VMEM((n_row, blk, wide), BF16),
                pltpu.VMEM((n_row - 1, blk, wide), BF16),
                pltpu.VMEM((blk, wide), BF16),
                pltpu.VMEM((n_dp, blk, wide), BF16),
                pltpu.SemaphoreType.DMA((2,)),
                pltpu.SemaphoreType.DMA((3,)),
                pltpu.SemaphoreType.DMA((steps,)),
                pltpu.SemaphoreType.DMA((22,)),
                pltpu.SemaphoreType.DMA((22,)),
                pltpu.SemaphoreType.DMA((11,)),
                pltpu.SemaphoreType.DMA((11,)),
            ],
            compiler_params=pltpu.CompilerParams(
                collective_id=0, has_side_effects=True, vmem_limit_bytes=60 * 2**20),
            name="mlp_step",
        )(x_dev.transpose(0, 2, 1), dy_dev.transpose(0, 2, 1), gate.T, up_w.T, down, g_dev[0])
        return dx_t.transpose(0, 2, 1), gn.transpose(0, 2, 1), dw[None]

    in_specs = (P(None, TOK_AXES, None), P(None, TOK_AXES, None), P(None, GROUP_AXES), P(None, GROUP_AXES), P(GROUP_AXES, None), P(TOK_AXES, None, None, None))
    out_specs = (P(None, TOK_AXES, None), P(None, None, GROUP_AXES), P(TOK_AXES, None, None, None))
    return jax.shard_map(local_step, mesh=mesh, in_specs=in_specs, out_specs=out_specs, check_vma=False)
```

time: 193 us -> 54.3 us (0.28)
  blocking collectives: 73.5 us -> 0 us
  matrix products: 51.6 us -> 0 us
  Pallas kernels: 0 us -> 47.8 us
  waiting for transfers between devices: 34 us -> 0 us
  between operations: 14.8 us -> 0.66 us
  local copies, waits for them, and re-layouts: 12.5 us -> 5.67 us
  other arithmetic: 4.72 us -> 0 us
    all_gather x3 -> x0, blocking collectives: 73.5 us -> none  [the longest x1 26.6 us: local_step(): w_gate = lax.all_gather(gate_shard, GROUP_AXES, axis=1, tiled=True)]
    dot_general x8 -> x0, matrix products: 51.6 us -> none  [the longest x1 16.9 us: mlp_backward(): jnp.einsum('td,fd->tf', dy_flat, w_down, preferred_element_type=jnp.float32)]
    pallas_call x0 -> x1, Pallas kernels: none -> 47.8 us  [local_step(): pl.pallas_call(body, in_specs=[hbm, hbm, vmem, vmem, vmem, hbm], out_spec...]
    psum x1 -> x0, waiting for transfers between devices: 34 us -> none  [local_step(): grad_next = lax.psum(g_shard.astype(jnp.float32), 'dp')]
    reshape x3 -> x0, local copies, waits for them, and re-layouts: 4.95 us -> none  [the longest x1 1.82 us: local_step(): x_dev.reshape(micro_count * tok_dev, d_model)]
    broadcast_in_dim x1 -> x0, other arithmetic: 3.11 us -> none  [local_step(): grad_layer[None]]
    unnamed x19 -> x7, local copies, waits for them, and re-layouts: 7.54 us -> 5.67 us
  transfers between devices with their start and end apart: 2 -> 0, of which waited for: 1 -> 0; matrix products, arithmetic and copies ran while one was open for 32% -> 0% of each run, Pallas kernels for 0% -> 0%
where the time goes in v1:
time: 54.3 us; the launch traced here: 54.1 us
  Pallas kernels  47.8 us (88%)
  local copies, waits for them, and re-layouts  5.67 us (10%)
  between operations  0.66 us (1%)
    pallas_call x1, Pallas kernels, local_step(): pl.pallas_call(body, in_specs=[hbm, hbm, vmem, vmem, vmem, hbm], out_spec...  47.8 us
    unnamed x7, local copies, waits for them, and re-layouts  5.67 us

profile of v1, /device:TPU:1, one launch (start us, length us, event | category | flops | bytes accessed | tf_op | source)
XLA Modules:
  0.0 54.1 jit_solution(2401085403095599559)
XLA Ops:
  0.6 47.8 %mlp_step.1 = (bf16[2,288,2048]{2,1,0:T(8,128)(2,1)}, f32[3,24,288]{2,1,0:T(8,128)}, f32[3,288,768]{2,1,0:T(8,128)}) custom-call(bf16[2,288,2048]{2,1,0:T(8,128)(2,1)} %bitcast.11, bf16[2,288,2048]{2,1,0:T(8,128)(2,1)} %bitcast.12, bf16[24,288]{1,0:T(8,128)(2,1)} %bitcast.14, bf16[24,288]{1,0:T(8,128)(2,1)} %bitcast.15, bf16[24,288]{1,0:T(8,128)(2,1)} %refs_4_.1, ...), custom_call_target="tpu_custom_call" | custom-call | tf_op jit(solution)/shard_map/mlp_step/pallas_call | solution.py:248
  48.4 0.0 copy-start.1
  48.4 0.0 copy-start
  48.4 3.5 %copy.12 = bf16[2,2048,288]{1,2,0:T(8,128)(2,1)} copy(bf16[2,2048,288]{1,2,0:T(8,128)(2,1)} %bitcast.10) | data formatting | bytes 4718592
  51.9 0.0 copy-done.1
  51.9 0.6 %copy.13 = f32[3,288,24]{1,2,0:T(8,128)} copy(f32[3,288,24]{1,2,0:T(8,128)S(1)} %bitcast.13) | data formatting | bytes 165888
  52.6 0.0 copy-done
  52.6 1.5 %copy.14 = f32[1,3,288,768]{3,2,1,0:T(8,128)} copy(f32[1,3,288,768]{3,2,1,0:T(8,128)S(1)} %bitcast.8) | data formatting | bytes 5308416
Async XLA Ops:
  48.4 3.5 %copy-start.1 = (f32[3,24,288]{2,1,0:T(8,128)S(1)}, f32[3,24,288]{2,1,0:T(8,128)}, u32[]{:S(2)}) copy-start(f32[3,24,288]{2,1,0:T(8,128)} %get-tuple-element.7) | copy-start | bytes 248836
  48.4 4.2 %copy-start = (f32[3,288,768]{2,1,0:T(8,128)S(1)}, f32[3,288,768]{2,1,0:T(8,128)}, u32[]{:S(2)}) copy-start(f32[3,288,768]{2,1,0:T(8,128)} %get-tuple-element.8) | copy-start | bytes 7962628

commit v2 on v1

--- a/solution.py
+++ b/solution.py
@@ -19,12 +19,12 @@
 
 
 def kernel(n_dp, n_row, n_x, micro, tokens, d_model, ff, blk,
-           x_hbm, dy_hbm, w1_ref, w3_ref, w2_ref, g_hbm,
-           dx_hbm, gn_ref, dw_hbm,
-           x_v, dy_v, dx_v, acc, g_v,
+           x_hbm, dy_hbm, w1_hbm, w3_hbm, w2_hbm, g_hbm,
+           dx_v, gn_ref, acc,
+           x_v, dy_v, g_v, shard,
            wa, wb, w1t, w3t, w2t, w1, w3,
            gt, pr, part, rx1, up, rx2, q, ry, r, rz,
-           load_sem, g_sem, out_sem, ag_s, ag_r, rs_s, rs_r):
+           load_sem, g_sem, ag_s, ag_r, rs_s, rs_r):
     z, y, f = lax.axis_index("dp"), lax.axis_index("row"), lax.axis_index("fsdp")
     x, c = f // 2, f % 2
     main, tail = 256, d_model - 256
@@ -49,10 +49,13 @@
     g_loads = [pltpu.make_async_copy(g_hbm.at[s], g_v.at[s], g_sem.at[s]) for s in range(3)]
     x_load = pltpu.make_async_copy(x_hbm, x_v, load_sem.at[0])
     dy_load = pltpu.make_async_copy(dy_hbm, dy_v, load_sem.at[1])
-    for load in g_loads + [x_load, dy_load]:
+    w_loads = [pltpu.make_async_copy(w, shard.at[i], load_sem.at[2 + i]) for i, w in enumerate((w1_hbm, w3_hbm, w2_hbm))]
+    for load in w_loads + g_loads + [x_load, dy_load]:
         load.start()
-
-    s1, s3, s2 = w1_ref[...], w3_ref[...], w2_ref[...]
+    for load in w_loads:
+        load.wait()
+
+    s1, s3, s2 = shard[0], shard[1], shard[2]
     wa[y, x, c, :, :main] = s1[:, :main]
     wa[y, x, c, :, main:] = s3[:, :main]
     wb[y, x, c, :, :main] = s2[:, :main]
@@ -170,11 +173,6 @@
         up[1, :hy] = part[:hy, xm]
         up[1, hy:] = (part[hy:, xm].astype(F32) + rx1[1].astype(F32)).astype(BF16)
 
-    def out_copy(i):
-        m, t = i // per, i % per
-        where = pl.ds(pl.multiple_of(t * TILE, TILE), TILE)
-        return pltpu.make_async_copy(dx_v.at[m, :, where], dx_hbm.at[m, :, where], out_sem.at[i])
-
     def step(i, carry):
         m, t = i // per, i % per
         where = pl.ds(pl.multiple_of(t * TILE, TILE), TILE)
@@ -189,7 +187,6 @@
         acc[0] += mm(xt, da, NT)
         acc[1] += mm(xt, db, NT)
         acc[2] += mm(dyt, h, NT)
-        out_copy(i).start()
         return carry
 
     quarter = steps // 4
@@ -211,9 +208,6 @@
     zs = [send("rs", r, rz.at[z], at_z(d)) for d in range(1, n_dp)]
     rz[z] = r[...]
     lax.fori_loop(3 * quarter, steps, step, 0)
-    dw_out = [pltpu.make_async_copy(acc.at[s], dw_hbm.at[s], g_sem.at[s]) for s in range(3)]
-    for copy in dw_out:
-        copy.start()
     for copy in zs:
         copy.wait_recv()
     total = rz[0].astype(F32)
@@ -224,10 +218,16 @@
         gn_ref[s, :, main:] = total[:, 3 * main + s * tail:3 * main + (s + 1) * tail]
     for copy in sent:
         copy.wait_send()
-    for copy in dw_out:
+
+
+def write_out(*refs):
+    n = len(refs) // 2
+    sems = refs[-1]
+    copies = [pltpu.make_async_copy(refs[i], refs[n + i], sems.at[i]) for i in range(n)]
+    for copy in copies:
+        copy.start()
+    for copy in copies:
         copy.wait()
-    for i in range(steps):
-        out_copy(i).wait()
 
 
 def solution(mesh):
@@ -244,22 +244,19 @@
         def body(*refs):
             kernel(n_dp, n_row, n_x, micro, tokens, d_model, ff, blk, *refs)
 
-        steps = micro * (tokens // TILE)
-        dx_t, gn, dw = pl.pallas_call(
+        shapes = [((micro, d_model, tokens), BF16), ((3, blk, d_model), F32), ((3, d_model, ff), F32)]
+        args = [x_dev.transpose(0, 2, 1), dy_dev.transpose(0, 2, 1), gate.T, up_w.T, down, g_dev[0]]
+        args = [pltpu.with_memory_space_constraint(arg, pltpu.HBM) for arg in args]
+        parts = pl.pallas_call(
             body,
-            in_specs=[hbm, hbm, vmem, vmem, vmem, hbm],
-            out_specs=[hbm, vmem, hbm],
-            out_shape=[
-                jax.ShapeDtypeStruct((micro, d_model, tokens), BF16),
-                jax.ShapeDtypeStruct((3, blk, d_model), F32),
-                jax.ShapeDtypeStruct((3, d_model, ff), F32),
-            ],
+            in_specs=[hbm] * 6,
+            out_specs=[vmem] * 3,
+            out_shape=[pltpu.VMEM(*shape) for shape in shapes],
             scratch_shapes=[
                 pltpu.VMEM((micro, d_model, tokens), BF16),
                 pltpu.VMEM((micro, d_model, tokens), BF16),
-                pltpu.VMEM((micro, d_model, tokens), BF16),
                 pltpu.VMEM((3, d_model, ff), F32),
-                pltpu.VMEM((3, d_model, ff), F32),
+                pltpu.VMEM((3, blk, d_model), BF16),
                 pltpu.VMEM((n_row, n_x, 2, blk, 512), BF16),
                 pltpu.VMEM((n_row, n_x, 2, blk, 384), BF16),
                 pltpu.VMEM((ff, d_model), BF16),
@@ -277,18 +274,26 @@
                 pltpu.VMEM((n_row - 1, blk, wide), BF16),
                 pltpu.VMEM((blk, wide), BF16),
                 pltpu.VMEM((n_dp, blk, wide), BF16),
-                pltpu.SemaphoreType.DMA((2,)),
+                pltpu.SemaphoreType.DMA((5,)),
                 pltpu.SemaphoreType.DMA((3,)),
-                pltpu.SemaphoreType.DMA((steps,)),
                 pltpu.SemaphoreType.DMA((22,)),
                 pltpu.SemaphoreType.DMA((22,)),
                 pltpu.SemaphoreType.DMA((11,)),
                 pltpu.SemaphoreType.DMA((11,)),
             ],
             compiler_params=pltpu.CompilerParams(
-                collective_id=0, has_side_effects=True, vmem_limit_bytes=60 * 2**20),
+                collective_id=0, has_side_effects=True, vmem_limit_bytes=44 * 2**20),
             name="mlp_step",
-        )(x_dev.transpose(0, 2, 1), dy_dev.transpose(0, 2, 1), gate.T, up_w.T, down, g_dev[0])
+        )(*args)
+        dx_t, gn, dw = pl.pallas_call(
+            write_out,
+            in_specs=[vmem] * 3,
+            out_specs=[hbm] * 3,
+            out_shape=[jax.ShapeDtypeStruct(*shape) for shape in shapes],
+            scratch_shapes=[pltpu.SemaphoreType.DMA((3,))],
+            compiler_params=pltpu.CompilerParams(vmem_limit_bytes=2 * 2**20),
+            name="write_out",
+        )(*parts)
         return dx_t.transpose(0, 2, 1), gn.transpose(0, 2, 1), dw[None]
 
     in_specs = (P(None, TOK_AXES, None), P(None, TOK_AXES, None), P(None, GROUP_AXES), P(None, GROUP_AXES), P(GROUP_AXES, None), P(TOK_AXES, None, None, None))

time: 54.3 us -> 48.4 us (0.89)
  local copies, waits for them, and re-layouts: 5.67 us -> 0 us
    unnamed x7 -> x0, local copies, waits for them, and re-layouts: 5.67 us -> none
    pallas_call x1 -> x2, Pallas kernels: 47.8 us -> 47.6 us  [the longest x1 45.3 us: local_step(): pl.pallas_call(body, in_specs=[hbm] * 6, out_specs=[vmem] * 3, out_shape=...]
where the time goes in v2:
time: 48.4 us; the launch traced here: 48.3 us
  Pallas kernels  47.6 us (98%)
  between operations  0.64 us (1%)
    pallas_call x1, Pallas kernels, local_step(): pl.pallas_call(body, in_specs=[hbm] * 6, out_specs=[vmem] * 3, out_shape=...  45.3 us
    pallas_call x1, Pallas kernels, local_step(): pl.pallas_call(write_out, in_specs=[vmem] * 3, out_specs=[hbm] * 3, out_s...  2.34 us

profile of v2, /device:TPU:1, one launch (start us, length us, event | category | flops | bytes accessed | tf_op | source)
XLA Modules:
  0.0 48.3 jit_solution(15505287598825877059)
XLA Ops:
  0.6 45.3 %mlp_step.1 = (bf16[2,288,2048]{2,1,0:T(8,128)(2,1)S(1)}, f32[3,24,288]{2,1,0:T(8,128)S(1)}, f32[3,288,768]{2,1,0:T(8,128)S(1)}) custom-call(bf16[2,288,2048]{2,1,0:T(8,128)(2,1)} %bitcast.9, bf16[2,288,2048]{2,1,0:T(8,128)(2,1)} %bitcast.10, bf16[24,288]{1,0:T(8,128)(2,1)} %bitcast.11, bf16[24,288]{1,0:T(8,128)(2,1)} %bitcast.12, bf16[24,288]{1,0:T(8,128)(2,1)} %refs_4_.1, ...), custom_call_target="tpu_custom_call" | custom-call | tf_op jit(solution)/shard_map/mlp_step/pallas_call | solution.py:250
  45.9 2.3 %write_out.1 = (bf16[2,288,2048]{2,1,0:T(8,128)(2,1)}, f32[3,24,288]{2,1,0:T(8,128)}, f32[3,288,768]{2,1,0:T(8,128)}) custom-call(bf16[2,288,2048]{2,1,0:T(8,128)(2,1)S(1)} %get-tuple-element.9.refs_0_, f32[3,24,288]{2,1,0:T(8,128)S(1)} %get-tuple-element.10.refs_1_, f32[3,288,768]{2,1,0:T(8,128)S(1)} %get-tuple-element.11.refs_2_), custom_call_target="tpu_custom_call" | custom-call | tf_op jit(solution)/shard_map/write_out/pallas_call | solution.py:288

commit v3 on v2

v3 whole, which is shorter than its diff:
```python
import jax
import jax.numpy as jnp
from jax import lax
from jax.experimental import pallas as pl
from jax.experimental.pallas import tpu as pltpu
from jax.sharding import PartitionSpec as P

TOK_AXES = ("dp", "row", "fsdp")
GROUP_AXES = ("row", "fsdp")
F32, BF16 = jnp.float32, jnp.bfloat16
MESH = pl.DeviceIdType.MESH
NN = (((1,), (0,)), ((), ()))
NT = (((1,), (1,)), ((), ()))


def mm(lhs, rhs, dims=NN):
    return lax.dot_general(lhs, rhs, dims, preferred_element_type=F32)


def kernel(n_dp, n_row, n_x, micro, tokens, d_model, ff, blk,
           x_hbm, dy_hbm, w1_hbm, w3_hbm, w2_hbm, g_hbm,
           dx_v, gn_ref, acc,
           x_v, dy_v, g_v, shard, wbuf, g1, g3, g2, w1, w3, hs, das, dbs,
           gt, pr, part, rx1, rx0, mid, rx2, q, ry, r, rz,
           load_sem, g_sem, ag_s, ag_r, rs_s, rs_r):
    z, y, f = lax.axis_index("dp"), lax.axis_index("row"), lax.axis_index("fsdp")
    x, c = f // 2, f % 2
    main, tail = 256, d_model - 256
    side = n_x
    rows = 2 * blk

    def chip(du, dv):
        return (y + dv * (1 - c) + du * c + side) % side, (x + du * (1 - c) + dv * c + side) % side

    def device(du, dv):
        yy, xx = chip(du, dv)
        return (z, yy, xx * 2 + c)

    def at_z(d):
        return ((z + d) % n_dp, y, f)

    partner = (z, y, x * 2 + 1 - c)
    peers = [partner, device(1, 0), device(-1, 0), device(0, 1), device(0, -1), device(0, 2)]
    peers += [at_z(d) for d in range(1, n_dp)]

    barrier = pltpu.get_barrier_semaphore()
    for peer in peers:
        pl.semaphore_signal(barrier, inc=1, device_id=peer, device_id_type=MESH)

    g_loads = [pltpu.make_async_copy(g_hbm.at[s], g_v.at[s], g_sem.at[s]) for s in range(3)]
    x_load = pltpu.make_async_copy(x_hbm, x_v, load_sem.at[0])
    dy_load = pltpu.make_async_copy(dy_hbm, dy_v, load_sem.at[1])
    w_loads = [pltpu.make_async_copy(w, shard.at[i], load_sem.at[2 + i]) for i, w in enumerate((w1_hbm, w3_hbm, w2_hbm))]
    for load in w_loads + g_loads + [x_load, dy_load]:
        load.start()
    for load in w_loads:
        load.wait()

    s1, s3, s2 = shard[0], shard[1], shard[2]
    wbuf[y, x, c, :, :main] = s1[:, :main]
    wbuf[y, x, c, :, main:2 * main] = s3[:, :main]
    wbuf[y, x, c, :, 2 * main:3 * main] = s2[:, :main]
    tails = [s[:, main:].astype(F32) for s in (s1, s3, s2)] + [jnp.zeros((blk, 128 - 3 * tail), F32)]
    wbuf[y, x, c, :, 3 * main:] = jnp.concatenate(tails, axis=1).astype(BF16)

    pl.semaphore_wait(barrier, len(peers))

    sent = []
    count = {"ag": 0, "rs": 0}

    def send(kind, src, dst, where):
        i = count[kind]
        count[kind] += 1
        ss, rr = (ag_s, ag_r) if kind == "ag" else (rs_s, rs_r)
        copy = pltpu.make_async_remote_copy(
            src_ref=src, dst_ref=dst, send_sem=ss.at[i], recv_sem=rr.at[i],
            device_id=where, device_id_type=MESH)
        copy.start()
        sent.append(copy)
        return copy

    arrive, pairs = {}, {}

    def forward(du, dv, su, sv):
        ref = wbuf.at[(*chip(du, dv), c)]
        got = tuple((a - b + 1) % side - 1 for a, b in ((du, su), (dv, sv)))
        arrive[got] = send("ag", ref, ref, device(su, sv))

    def share(du, dv):
        ref = wbuf.at[(*chip(du, dv), c)]
        pairs[du, dv] = send("ag", ref, ref, partner)

    def take(du, dv, *steps):
        arrive[du, dv].wait_recv()
        for su, sv in steps:
            forward(du, dv, su, sv)
        share(du, dv)

    for su, sv in ((1, 0), (-1, 0), (0, 1), (0, -1)):
        forward(0, 0, su, sv)
    share(0, 0)

    def turn(s):
        g_loads[s].wait()
        flat = g_v[s, :main, :].T.reshape(n_row, n_x, 2, blk, main)
        gt[..., s * main:(s + 1) * main] = flat.astype(BF16)

    def turn_tail():
        parts = [g_v[s, main:, :] for s in range(3)] + [jnp.zeros((128 - 3 * tail, ff), F32)]
        flat = jnp.concatenate(parts, axis=0).T.reshape(n_row, n_x, 2, blk, 128)
        gt[..., 3 * main:] = flat.astype(BF16)

    def fill(group):
        for j, (du, dv) in enumerate(group):
            both = wbuf[chip(du, dv)].astype(F32).reshape(rows, 3 * main + 128).astype(BF16)
            at = slice(j * rows, (j + 1) * rows)
            for i, ref in enumerate((g1, g3, g2)):
                ref[at, :main] = both[:, i * main:(i + 1) * main]
                ref[at, main:] = both[:, 3 * main + i * tail:3 * main + (i + 1) * tail]

    def ahead(group, m):
        n = len(group) * rows
        to = pl.ds(pl.multiple_of(m * tokens, tokens), tokens)
        xt, dyt = x_v[m], dy_v[m]
        a, b, dh = mm(g1[:n], xt), mm(g3[:n], xt), mm(g2[:n], dyt)
        sig = 0.5 * jnp.tanh(0.5 * a) + 0.5
        act = a * sig
        h = (act * b).astype(BF16)
        db = (dh * act).astype(BF16)
        da = (dh * b * (sig + act * (1.0 - sig))).astype(BF16)
        for j, (du, dv) in enumerate(group):
            yy, xx = chip(du, dv)
            first = pl.multiple_of((yy * n_x + xx) * rows, 16)
            at = slice(j * rows, (j + 1) * rows)
            hs[pl.ds(first, rows), to] = h[at]
            das[pl.ds(first, rows), to] = da[at]
            dbs[pl.ds(first, rows), to] = db[at]

    def back(m):
        to = pl.ds(pl.multiple_of(m * tokens, tokens), tokens)
        xt, dyt = x_v[m], dy_v[m]
        h, da, db = hs[:, to], das[:, to], dbs[:, to]
        dx_v[m] = (mm(w1[...], da) + mm(w3[...], db)).astype(BF16)
        acc[0] += mm(xt, da, NT)
        acc[1] += mm(xt, db, NT)
        acc[2] += mm(dyt, h, NT)

    turn(0)
    turn(1)
    turn(2)
    turn_tail()
    pair = send("rs", gt.at[:, :, 1 - c], pr, partner)
    acc[...] = jnp.zeros_like(acc)
    x_load.wait()
    dy_load.wait()
    pairs[0, 0].wait_recv()
    fill([(0, 0)])
    ahead([(0, 0)], 0)

    take(-1, 0, (1, 0), (0, 1), (0, -1))
    take(1, 0, (0, 1), (0, -1))
    take(0, -1, (0, 1))
    take(0, 1)
    pair.wait_recv()
    for yy in range(n_row):
        for xx in range(n_x):
            both = gt[yy, xx, c].astype(F32) + pr[yy, xx].astype(F32)
            part[xx * (1 - c) + yy * c, yy * (1 - c) + xx * c] = both.astype(BF16)
    u, v = x * (1 - c) + y * c, y * (1 - c) + x * c
    um, up, uo = (u + side - 1) % side, (u + 1) % side, (u + 2) % side
    lo, hi = pl.ds(0, side // 2), pl.ds(side // 2, side // 2)

    u1 = [send("rs", part.at[uo, lo], rx1.at[0], device(1, 0)),
          send("rs", part.at[uo, hi], rx1.at[1], device(-1, 0))]
    u0 = [send("rs", part.at[up, hi], rx0.at[0], device(1, 0)),
          send("rs", part.at[um, lo], rx0.at[1], device(-1, 0))]
    ahead([(0, 0)], 1)
    near = [(-1, 0), (1, 0), (0, -1), (0, 1)]
    for key in near:
        pairs[key].wait_recv()
    fill(near)
    ahead(near, 0)
    take(2, 0, (0, 1), (0, -1))
    take(-1, -1, (0, 1))
    take(1, 1, (0, -1))
    take(-1, 1)
    take(1, -1)
    take(0, 2)
    ahead(near, 1)
    mids = [(2, 0), (0, 2), (-1, -1), (1, 1), (-1, 1), (1, -1)]
    for key in mids:
        pairs[key].wait_recv()
    fill(mids)
    ahead(mids, 0)
    take(2, 1, (0, -1))
    take(2, -1)
    take(-1, 2)
    take(1, 2)
    ahead(mids, 1)

    for copy in u1:
        copy.wait_recv()
    half = side // 2
    mid[0] = (part[up, :half].astype(F32) + rx1[0].astype(F32)).astype(BF16)
    mid[1] = (part[um, half:].astype(F32) + rx1[1].astype(F32)).astype(BF16)
    u2 = [send("rs", mid.at[0], rx2.at[0], device(1, 0)), send("rs", mid.at[1], rx2.at[1], device(-1, 0))]

    far = [(2, 1), (2, -1), (-1, 2), (1, 2)]
    for key in far:
        pairs[key].wait_recv()
    fill(far)
    ahead(far, 0)
    take(2, 2)
    ahead(far, 1)
    pairs[2, 2].wait_recv()
    fill([(2, 2)])

    for copy in u0 + u2:
        copy.wait_recv()
    q[:half] = (part[u, :half].astype(F32) + rx2[0].astype(F32) + rx0[1].astype(F32)).astype(BF16)
    q[half:] = (part[u, half:].astype(F32) + rx2[1].astype(F32) + rx0[0].astype(F32)).astype(BF16)
    vs = [send("rs", q.at[(v + d) % side], ry.at[d - 1], device(0, d)) for d in (2, 1, 3)]

    def across(lo, hi):
        return wbuf[..., lo:hi].astype(F32).reshape(ff, hi - lo).astype(BF16).T

    w1[:main, :] = across(0, main)
    w3[:main, :] = across(main, 2 * main)
    ends = across(3 * main, 3 * main + 128)
    w1[main:, :] = ends[:tail]
    w3[main:, :] = ends[tail:2 * tail]

    ahead([(2, 2)], 0)
    back(0)
    for copy in vs:
        copy.wait_recv()
    own = q[v].astype(F32)
    for d in range(1, side):
        own += ry[d - 1].astype(F32)
    r[...] = own.astype(BF16)
    zs = [send("rs", r, rz.at[z], at_z(d)) for d in (2, 1, 3)]
    rz[z] = r[...]
    ahead([(2, 2)], 1)
    back(1)
    for copy in zs:
        copy.wait_recv()
    total = rz[0].astype(F32)
    for d in range(1, n_dp):
        total += rz[d].astype(F32)
    for s in range(3):
        gn_ref[s, :, :main] = total[:, s * main:(s + 1) * main]
        gn_ref[s, :, main:] = total[:, 3 * main + s * tail:3 * main + (s + 1) * tail]
    for copy in sent:
        copy.wait_send()


def write_out(*refs):
    n = len(refs) // 2
    sems = refs[-1]
    copies = [pltpu.make_async_copy(refs[i], refs[n + i], sems.at[i]) for i in range(n)]
    for copy in copies:
        copy.start()
    for copy in copies:
        copy.wait()


def solution(mesh):
    n_dp, n_row, n_x = mesh.shape["dp"], mesh.shape["row"], mesh.shape["fsdp"] // 2

    def local_step(x_dev, dy_dev, gate, up_w, down, g_dev):
        micro, tokens, d_model = x_dev.shape
        blk = gate.shape[1]
        ff = blk * n_row * n_x * 2
        wide = 3 * 256 + 128
        vmem = pl.BlockSpec(memory_space=pltpu.VMEM)
        hbm = pl.BlockSpec(memory_space=pltpu.HBM)

        def body(*refs):
            kernel(n_dp, n_row, n_x, micro, tokens, d_model, ff, blk, *refs)

        shapes = [((micro, d_model, tokens), BF16), ((3, blk, d_model), F32), ((3, d_model, ff), F32)]
        args = [x_dev.transpose(0, 2, 1), dy_dev.transpose(0, 2, 1), gate.T, up_w.T, down, g_dev[0]]
        args = [pltpu.with_memory_space_constraint(arg, pltpu.HBM) for arg in args]
        parts = pl.pallas_call(
            body,
            in_specs=[hbm] * 6,
            out_specs=[vmem] * 3,
            out_shape=[pltpu.VMEM(*shape) for shape in shapes],
            scratch_shapes=[
                pltpu.VMEM((micro, d_model, tokens), BF16),
                pltpu.VMEM((micro, d_model, tokens), BF16),
                pltpu.VMEM((3, d_model, ff), F32),
                pltpu.VMEM((3, blk, d_model), BF16),
                pltpu.VMEM((n_row, n_x, 2, blk, wide), BF16),
                pltpu.VMEM((12 * blk, d_model), BF16),
                pltpu.VMEM((12 * blk, d_model), BF16),
                pltpu.VMEM((12 * blk, d_model), BF16),
                pltpu.VMEM((d_model, ff), BF16),
                pltpu.VMEM((d_model, ff), BF16),
                pltpu.VMEM((ff, micro * tokens), BF16),
                pltpu.VMEM((ff, micro * tokens), BF16),
                pltpu.VMEM((ff, micro * tokens), BF16),
                pltpu.VMEM((n_row, n_x, 2, blk, wide), BF16),
                pltpu.VMEM((n_row, n_x, blk, wide), BF16),
                pltpu.VMEM((n_row, n_x, blk, wide), BF16),
                pltpu.VMEM((2, 2, blk, wide), BF16),
                pltpu.VMEM((2, 2, blk, wide), BF16),
                pltpu.VMEM((2, 2, blk, wide), BF16),
                pltpu.VMEM((2, 2, blk, wide), BF16),
                pltpu.VMEM((4, blk, wide), BF16),
                pltpu.VMEM((3, blk, wide), BF16),
                pltpu.VMEM((blk, wide), BF16),
                pltpu.VMEM((n_dp, blk, wide), BF16),
                pltpu.SemaphoreType.DMA((5,)),
                pltpu.SemaphoreType.DMA((3,)),
                pltpu.SemaphoreType.DMA((31,)),
                pltpu.SemaphoreType.DMA((31,)),
                pltpu.SemaphoreType.DMA((13,)),
                pltpu.SemaphoreType.DMA((13,)),
            ],
            compiler_params=pltpu.CompilerParams(
                collective_id=0, has_side_effects=True, vmem_limit_bytes=54 * 2**20),
            name="mlp_step",
        )(*args)
        dx_t, gn, dw = pl.pallas_call(
            write_out,
            in_specs=[vmem] * 3,
            out_specs=[hbm] * 3,
            out_shape=[jax.ShapeDtypeStruct(*shape) for shape in shapes],
            scratch_shapes=[pltpu.SemaphoreType.DMA((3,))],
            compiler_params=pltpu.CompilerParams(vmem_limit_bytes=2 * 2**20),
            name="write_out",
        )(*parts)
        return dx_t.transpose(0, 2, 1), gn.transpose(0, 2, 1), dw[None]

    in_specs = (P(None, TOK_AXES, None), P(None, TOK_AXES, None), P(None, GROUP_AXES), P(None, GROUP_AXES), P(GROUP_AXES, None), P(TOK_AXES, None, None, None))
    out_specs = (P(None, TOK_AXES, None), P(None, None, GROUP_AXES), P(TOK_AXES, None, None, None))
    return jax.shard_map(local_step, mesh=mesh, in_specs=in_specs, out_specs=out_specs, check_vma=False)
```

time: 48.4 us -> 43.2 us (0.89)
  Pallas kernels: 47.6 us -> 41.9 us
    pallas_call x1, Pallas kernels: 45.3 us -> 39.5 us  [local_step(): pl.pallas_call(body, in_specs=[hbm] * 6, out_specs=[vmem] * 3, out_shape=...]
where the time goes in v3:
time: 43.2 us; the launch traced here: 42.7 us
  Pallas kernels  41.9 us (97%)
  between operations  0.8 us (2%)
    pallas_call x1, Pallas kernels, local_step(): pl.pallas_call(body, in_specs=[hbm] * 6, out_specs=[vmem] * 3, out_shape=...  39.5 us
    pallas_call x1, Pallas kernels, local_step(): pl.pallas_call(write_out, in_specs=[vmem] * 3, out_specs=[hbm] * 3, out_s...  2.34 us

profile of v3, /device:TPU:1, one launch (start us, length us, event | category | flops | bytes accessed | tf_op | source)
XLA Modules:
  0.0 42.7 jit_solution(11819005561647753717)
XLA Ops:
  0.6 39.5 %mlp_step.1 = (bf16[2,288,2048]{2,1,0:T(8,128)(2,1)S(1)}, f32[3,24,288]{2,1,0:T(8,128)S(1)}, f32[3,288,768]{2,1,0:T(8,128)S(1)}) custom-call(bf16[2,288,2048]{2,1,0:T(8,128)(2,1)} %bitcast.9, bf16[2,288,2048]{2,1,0:T(8,128)(2,1)} %bitcast.10, bf16[24,288]{1,0:T(8,128)(2,1)} %bitcast.11, bf16[24,288]{1,0:T(8,128)(2,1)} %bitcast.12, bf16[24,288]{1,0:T(8,128)(2,1)} %refs_4_.1, ...), custom_call_target="tpu_custom_call" | custom-call | tf_op jit(solution)/shard_map/mlp_step/pallas_call | solution.py:284
  40.2 2.3 %write_out.1 = (bf16[2,288,2048]{2,1,0:T(8,128)(2,1)}, f32[3,24,288]{2,1,0:T(8,128)}, f32[3,288,768]{2,1,0:T(8,128)}) custom-call(bf16[2,288,2048]{2,1,0:T(8,128)(2,1)S(1)} %get-tuple-element.9.refs_0_, f32[3,24,288]{2,1,0:T(8,128)S(1)} %get-tuple-element.10.refs_1_, f32[3,288,768]{2,1,0:T(8,128)S(1)} %get-tuple-element.11.refs_2_), custom_call_target="tpu_custom_call" | custom-call | tf_op jit(solution)/shard_map/write_out/pallas_call | solution.py:325

commit v4 on v3

--- a/solution.py
+++ b/solution.py
@@ -19,9 +19,9 @@
 
 def kernel(n_dp, n_row, n_x, micro, tokens, d_model, ff, blk,
            x_hbm, dy_hbm, w1_hbm, w3_hbm, w2_hbm, g_hbm,
-           dx_v, gn_ref, acc,
-           x_v, dy_v, g_v, shard, wbuf, g1, g3, g2, w1, w3, hs, das, dbs,
-           gt, pr, part, rx1, rx0, mid, rx2, q, ry, r, rz,
+           dx0, acc, x1, dy1, h1, da1, db1, w1, w3, r,
+           x0, dy0, h0, da0, db0, g_v, shard, wbuf, g1, g3, g2,
+           gt, pr, part, rx1, rx0, mid, rx2, q, ry,
            load_sem, g_sem, ag_s, ag_r, rs_s, rs_r):
     z, y, f = lax.axis_index("dp"), lax.axis_index("row"), lax.axis_index("fsdp")
     x, c = f // 2, f % 2
@@ -36,22 +36,18 @@
         yy, xx = chip(du, dv)
         return (z, yy, xx * 2 + c)
 
-    def at_z(d):
-        return ((z + d) % n_dp, y, f)
-
     partner = (z, y, x * 2 + 1 - c)
-    peers = [partner, device(1, 0), device(-1, 0), device(0, 1), device(0, -1), device(0, 2)]
-    peers += [at_z(d) for d in range(1, n_dp)]
+    peers = [partner, device(1, 0), device(-1, 0), device(0, 1), device(0, -1), device(0, 2), device(2, 0)]
 
     barrier = pltpu.get_barrier_semaphore()
     for peer in peers:
         pl.semaphore_signal(barrier, inc=1, device_id=peer, device_id_type=MESH)
 
     g_loads = [pltpu.make_async_copy(g_hbm.at[s], g_v.at[s], g_sem.at[s]) for s in range(3)]
-    x_load = pltpu.make_async_copy(x_hbm, x_v, load_sem.at[0])
-    dy_load = pltpu.make_async_copy(dy_hbm, dy_v, load_sem.at[1])
-    w_loads = [pltpu.make_async_copy(w, shard.at[i], load_sem.at[2 + i]) for i, w in enumerate((w1_hbm, w3_hbm, w2_hbm))]
-    for load in w_loads + g_loads + [x_load, dy_load]:
+    t_loads = [[pltpu.make_async_copy(src.at[m], dst[m], load_sem.at[3 + 2 * m + i])
+                for i, (src, dst) in enumerate(((x_hbm, (x0, x1)), (dy_hbm, (dy0, dy1))))] for m in range(micro)]
+    w_loads = [pltpu.make_async_copy(w, shard.at[i], load_sem.at[i]) for i, w in enumerate((w1_hbm, w3_hbm, w2_hbm))]
+    for load in w_loads + t_loads[0] + g_loads + t_loads[1]:
         load.start()
     for load in w_loads:
         load.wait()
@@ -96,7 +92,7 @@
             forward(du, dv, su, sv)
         share(du, dv)
 
-    for su, sv in ((1, 0), (-1, 0), (0, 1), (0, -1)):
+    for su, sv in ((1, 0), (-1, 0), (0, 1), (0, -1), (2, 0)):
         forward(0, 0, su, sv)
     share(0, 0)
 
@@ -118,10 +114,10 @@
                 ref[at, :main] = both[:, i * main:(i + 1) * main]
                 ref[at, main:] = both[:, 3 * main + i * tail:3 * main + (i + 1) * tail]
 
-    def ahead(group, m):
+    def ahead(group, m, lo=0, hi=tokens):
         n = len(group) * rows
-        to = pl.ds(pl.multiple_of(m * tokens, tokens), tokens)
-        xt, dyt = x_v[m], dy_v[m]
+        xt, dyt = ((x0, dy0), (x1, dy1))[m]
+        xt, dyt = xt[:, lo:hi], dyt[:, lo:hi]
         a, b, dh = mm(g1[:n], xt), mm(g3[:n], xt), mm(g2[:n], dyt)
         sig = 0.5 * jnp.tanh(0.5 * a) + 0.5
         act = a * sig
@@ -130,37 +126,36 @@
         da = (dh * b * (sig + act * (1.0 - sig))).astype(BF16)
         for j, (du, dv) in enumerate(group):
             yy, xx = chip(du, dv)
-            first = pl.multiple_of((yy * n_x + xx) * rows, 16)
+            to = pl.ds(pl.multiple_of((yy * n_x + xx) * rows, 16), rows)
             at = slice(j * rows, (j + 1) * rows)
-            hs[pl.ds(first, rows), to] = h[at]
-            das[pl.ds(first, rows), to] = da[at]
-            dbs[pl.ds(first, rows), to] = db[at]
-
-    def back(m):
-        to = pl.ds(pl.multiple_of(m * tokens, tokens), tokens)
-        xt, dyt = x_v[m], dy_v[m]
-        h, da, db = hs[:, to], das[:, to], dbs[:, to]
-        dx_v[m] = (mm(w1[...], da) + mm(w3[...], db)).astype(BF16)
-        acc[0] += mm(xt, da, NT)
-        acc[1] += mm(xt, db, NT)
-        acc[2] += mm(dyt, h, NT)
-
+            for ref, value in zip(((h0, da0, db0), (h1, da1, db1))[m], (h, da, db)):
+                ref[to, lo:hi] = value[at]
+
+    for load in t_loads[0]:
+        load.wait()
+    pairs[0, 0].wait_recv()
+    fill([(0, 0)])
+    ahead([(0, 0)], 0)
     turn(0)
     turn(1)
     turn(2)
     turn_tail()
+
+    take(-1, 0, (0, 1), (0, -1))
+    take(1, 0, (0, 1), (0, -1))
+    take(0, 1, (0, -1))
+    take(0, -1)
+    for load in t_loads[1]:
+        load.wait()
+    ahead([(0, 0)], 1)
+    near = [(-1, 0), (1, 0), (0, -1), (0, 1)]
+    take(2, 0, (0, 1), (0, -1))
+    for key in near:
+        pairs[key].wait_recv()
     pair = send("rs", gt.at[:, :, 1 - c], pr, partner)
-    acc[...] = jnp.zeros_like(acc)
-    x_load.wait()
-    dy_load.wait()
-    pairs[0, 0].wait_recv()
-    fill([(0, 0)])
-    ahead([(0, 0)], 0)
-
-    take(-1, 0, (1, 0), (0, 1), (0, -1))
-    take(1, 0, (0, 1), (0, -1))
-    take(0, -1, (0, 1))
-    take(0, 1)
+    fill(near)
+    ahead(near, 0)
+    ahead(near, 1, 0, tokens // 2)
     pair.wait_recv()
     for yy in range(n_row):
         for xx in range(n_x):
@@ -170,23 +165,14 @@
     um, up, uo = (u + side - 1) % side, (u + 1) % side, (u + 2) % side
     lo, hi = pl.ds(0, side // 2), pl.ds(side // 2, side // 2)
 
-    u1 = [send("rs", part.at[uo, lo], rx1.at[0], device(1, 0)),
-          send("rs", part.at[uo, hi], rx1.at[1], device(-1, 0))]
-    u0 = [send("rs", part.at[up, hi], rx0.at[0], device(1, 0)),
-          send("rs", part.at[um, lo], rx0.at[1], device(-1, 0))]
-    ahead([(0, 0)], 1)
-    near = [(-1, 0), (1, 0), (0, -1), (0, 1)]
-    for key in near:
-        pairs[key].wait_recv()
-    fill(near)
-    ahead(near, 0)
-    take(2, 0, (0, 1), (0, -1))
     take(-1, -1, (0, 1))
     take(1, 1, (0, -1))
     take(-1, 1)
     take(1, -1)
     take(0, 2)
-    ahead(near, 1)
+    u1 = [send("rs", part.at[uo, lo], rx1.at[0], device(1, 0)),
+          send("rs", part.at[uo, hi], rx1.at[1], device(-1, 0))]
+    ahead(near, 1, tokens // 2)
     mids = [(2, 0), (0, 2), (-1, -1), (1, 1), (-1, 1), (1, -1)]
     for key in mids:
         pairs[key].wait_recv()
@@ -196,6 +182,8 @@
     take(2, -1)
     take(-1, 2)
     take(1, 2)
+    u0 = [send("rs", part.at[up, hi], rx0.at[0], device(1, 0)),
+          send("rs", part.at[um, lo], rx0.at[1], device(-1, 0))]
     ahead(mids, 1)
 
     for copy in u1:
@@ -231,37 +219,47 @@
     w3[main:, :] = ends[tail:2 * tail]
 
     ahead([(2, 2)], 0)
-    back(0)
+    dx0[...] = (mm(w1[...], da0[...]) + mm(w3[...], db0[...])).astype(BF16)
+    acc[0] = mm(x0[...], da0[...], NT)
+    acc[1] = mm(x0[...], db0[...], NT)
+    acc[2] = mm(dy0[...], h0[...], NT)
+    ahead([(2, 2)], 1)
     for copy in vs:
         copy.wait_recv()
     own = q[v].astype(F32)
     for d in range(1, side):
         own += ry[d - 1].astype(F32)
     r[...] = own.astype(BF16)
-    zs = [send("rs", r, rz.at[z], at_z(d)) for d in (2, 1, 3)]
-    rz[z] = r[...]
-    ahead([(2, 2)], 1)
-    back(1)
-    for copy in zs:
-        copy.wait_recv()
-    total = rz[0].astype(F32)
-    for d in range(1, n_dp):
-        total += rz[d].astype(F32)
-    for s in range(3):
-        gn_ref[s, :, :main] = total[:, s * main:(s + 1) * main]
-        gn_ref[s, :, main:] = total[:, 3 * main + s * tail:3 * main + (s + 1) * tail]
     for copy in sent:
         copy.wait_send()
 
 
-def write_out(*refs):
-    n = len(refs) // 2
-    sems = refs[-1]
-    copies = [pltpu.make_async_copy(refs[i], refs[n + i], sems.at[i]) for i in range(n)]
-    for copy in copies:
-        copy.start()
-    for copy in copies:
-        copy.wait()
+def second(dx0, acc, x1, dy1, h1, da1, db1, w1, w3, dx_hbm, dw_hbm, dx1, dw, sems):
+    outs = [pltpu.make_async_copy(dx0, dx_hbm.at[0], sems.at[0]), pltpu.make_async_copy(dx1, dx_hbm.at[1], sems.at[1])]
+    outs += [pltpu.make_async_copy(dw.at[s], dw_hbm.at[s], sems.at[2 + s]) for s in range(3)]
+    outs[0].start()
+    dw[0] = acc[0] + mm(x1[...], da1[...], NT)
+    dw[1] = acc[1] + mm(x1[...], db1[...], NT)
+    dx1[...] = (mm(w1[...], da1[...]) + mm(w3[...], db1[...])).astype(BF16)
+    for i in (2, 3, 1):
+        outs[i].start()
+    dw[2] = acc[2] + mm(dy1[...], h1[...], NT)
+    outs[4].start()
+    for out in outs:
+        out.wait()
+
+
+def last(n_dp, main, tail, *refs):
+    parts, gn, stack = refs[:n_dp], refs[n_dp], refs[n_dp + 1]
+    z = lax.axis_index("dp")
+    for d in range(n_dp):
+        stack[(z + n_dp - d) % n_dp] = parts[d][...]
+    total = stack[0].astype(F32)
+    for d in range(1, n_dp):
+        total += stack[d].astype(F32)
+    for s in range(3):
+        gn[s, :, :main] = total[:, s * main:(s + 1) * main]
+        gn[s, :, main:] = total[:, 3 * main + s * tail:3 * main + (s + 1) * tail]
 
 
 def solution(mesh):
@@ -278,28 +276,28 @@
         def body(*refs):
             kernel(n_dp, n_row, n_x, micro, tokens, d_model, ff, blk, *refs)
 
-        shapes = [((micro, d_model, tokens), BF16), ((3, blk, d_model), F32), ((3, d_model, ff), F32)]
         args = [x_dev.transpose(0, 2, 1), dy_dev.transpose(0, 2, 1), gate.T, up_w.T, down, g_dev[0]]
         args = [pltpu.with_memory_space_constraint(arg, pltpu.HBM) for arg in args]
-        parts = pl.pallas_call(
+        half, mids = (d_model, tokens), (ff, tokens)
+        outs = [pltpu.VMEM(half, BF16), pltpu.VMEM((3, d_model, ff), F32)] + [pltpu.VMEM(half, BF16)] * 2
+        outs += [pltpu.VMEM(mids, BF16)] * 3 + [pltpu.VMEM((d_model, ff), BF16)] * 2 + [pltpu.VMEM((blk, wide), BF16)]
+        *rest, r = pl.pallas_call(
             body,
             in_specs=[hbm] * 6,
-            out_specs=[vmem] * 3,
-            out_shape=[pltpu.VMEM(*shape) for shape in shapes],
+            out_specs=[vmem] * len(outs),
+            out_shape=outs,
             scratch_shapes=[
-                pltpu.VMEM((micro, d_model, tokens), BF16),
-                pltpu.VMEM((micro, d_model, tokens), BF16),
+                pltpu.VMEM(half, BF16),
+                pltpu.VMEM(half, BF16),
+                pltpu.VMEM(mids, BF16),
+                pltpu.VMEM(mids, BF16),
+                pltpu.VMEM(mids, BF16),
                 pltpu.VMEM((3, d_model, ff), F32),
                 pltpu.VMEM((3, blk, d_model), BF16),
                 pltpu.VMEM((n_row, n_x, 2, blk, wide), BF16),
                 pltpu.VMEM((12 * blk, d_model), BF16),
                 pltpu.VMEM((12 * blk, d_model), BF16),
                 pltpu.VMEM((12 * blk, d_model), BF16),
-                pltpu.VMEM((d_model, ff), BF16),
-                pltpu.VMEM((d_model, ff), BF16),
-                pltpu.VMEM((ff, micro * tokens), BF16),
-                pltpu.VMEM((ff, micro * tokens), BF16),
-                pltpu.VMEM((ff, micro * tokens), BF16),
                 pltpu.VMEM((n_row, n_x, 2, blk, wide), BF16),
                 pltpu.VMEM((n_row, n_x, blk, wide), BF16),
                 pltpu.VMEM((n_row, n_x, blk, wide), BF16),
@@ -309,28 +307,41 @@
                 pltpu.VMEM((2, 2, blk, wide), BF16),
                 pltpu.VMEM((4, blk, wide), BF16),
                 pltpu.VMEM((3, blk, wide), BF16),
-                pltpu.VMEM((blk, wide), BF16),
-                pltpu.VMEM((n_dp, blk, wide), BF16),
-                pltpu.SemaphoreType.DMA((5,)),
+                pltpu.SemaphoreType.DMA((3 + 2 * micro,)),
                 pltpu.SemaphoreType.DMA((3,)),
                 pltpu.SemaphoreType.DMA((31,)),
                 pltpu.SemaphoreType.DMA((31,)),
-                pltpu.SemaphoreType.DMA((13,)),
-                pltpu.SemaphoreType.DMA((13,)),
+                pltpu.SemaphoreType.DMA((10,)),
+                pltpu.SemaphoreType.DMA((10,)),
             ],
             compiler_params=pltpu.CompilerParams(
-                collective_id=0, has_side_effects=True, vmem_limit_bytes=54 * 2**20),
+                collective_id=0, has_side_effects=True, vmem_limit_bytes=34 * 2**20),
             name="mlp_step",
         )(*args)
-        dx_t, gn, dw = pl.pallas_call(
-            write_out,
-            in_specs=[vmem] * 3,
-            out_specs=[hbm] * 3,
-            out_shape=[jax.ShapeDtypeStruct(*shape) for shape in shapes],
-            scratch_shapes=[pltpu.SemaphoreType.DMA((3,))],
-            compiler_params=pltpu.CompilerParams(vmem_limit_bytes=2 * 2**20),
-            name="write_out",
-        )(*parts)
+        ring = [r] + [lax.ppermute(r, "dp", [(i, (i + d) % n_dp) for i in range(n_dp)]) for d in range(1, n_dp)]
+        dx_t, dw = pl.pallas_call(
+            second,
+            in_specs=[vmem] * len(rest),
+            out_specs=[hbm] * 2,
+            out_shape=[jax.ShapeDtypeStruct((micro, d_model, tokens), BF16), jax.ShapeDtypeStruct((3, d_model, ff), F32)],
+            scratch_shapes=[pltpu.VMEM(half, BF16), pltpu.VMEM((3, d_model, ff), F32), pltpu.SemaphoreType.DMA((5,))],
+            compiler_params=pltpu.CompilerParams(vmem_limit_bytes=16 * 2**20),
+            cost_estimate=pl.CostEstimate(flops=7 * 10**9, bytes_accessed=5 * 10**6, transcendentals=0),
+            name="second",
+        )(*rest)
+
+        def finish(*refs):
+            last(n_dp, 256, d_model - 256, *refs)
+
+        gn = pl.pallas_call(
+            finish,
+            in_specs=[vmem] * n_dp,
+            out_specs=vmem,
+            out_shape=jax.ShapeDtypeStruct((3, blk, d_model), F32),
+            scratch_shapes=[pltpu.VMEM((n_dp, blk, wide), BF16)],
+            compiler_params=pltpu.CompilerParams(vmem_limit_bytes=4 * 2**20),
+            name="last_sum",
+        )(*ring)
         return dx_t.transpose(0, 2, 1), gn.transpose(0, 2, 1), dw[None]
 
     in_specs = (P(None, TOK_AXES, None), P(None, TOK_AXES, None), P(None, GROUP_AXES), P(None, GROUP_AXES), P(GROUP_AXES, None), P(TOK_AXES, None, None, None))

time: 43.2 us -> 42.9 us (level)
  starting transfers between devices: 0 us -> 4.51 us
  Pallas kernels: 41.9 us -> 37.4 us
    ppermute x0 -> x3, starting transfers between devices: none -> 4.51 us  [local_step(): lax.ppermute(r, 'dp', [(i, (i + d) % n_dp) for i in range(n_dp)])]
    pallas_call x2 -> x3, Pallas kernels: 41.9 us -> 37.4 us  [the longest x1 30.9 us: local_step(): pl.pallas_call(body, in_specs=[hbm] * 6, out_specs=[vmem] * len(outs), ou...]
  transfers between devices with their start and end apart: 0 -> 3, of which waited for: 0 -> 0; matrix products, arithmetic and copies ran while one was open for 0% -> 0% of each run, Pallas kernels for 0% -> 13%
where the time goes in v4:
time: 42.9 us; the launch traced here: 42.6 us
  Pallas kernels  37.4 us (87%)
  starting transfers between devices  4.51 us (11%)
  between operations  0.67 us (2%)
    pallas_call x1, Pallas kernels, local_step(): pl.pallas_call(body, in_specs=[hbm] * 6, out_specs=[vmem] * len(outs), ou...  30.9 us
    pallas_call x1, Pallas kernels, local_step(): pl.pallas_call(second, in_specs=[vmem] * len(rest), out_specs=[hbm] * 2,...  5.72 us
    ppermute x3, starting transfers between devices, local_step(): lax.ppermute(r, 'dp', [(i, (i + d) % n_dp) for i in range(n_dp)])  4.51 us
  transfers between devices with their start and end apart: 3, of which 0 were waited for; matrix products, arithmetic and copies ran while one was open for 0% of the time, Pallas kernels for 13%

profile of v4, /device:TPU:1, one launch (start us, length us, event | category | flops | bytes accessed | tf_op | source)
XLA Modules:
  0.0 42.6 jit_solution(14879306017368222101)
XLA Ops:
  0.6 30.9 %mlp_step.1 = (bf16[288,2048]{1,0:T(8,128)(2,1)S(1)}, f32[3,288,768]{2,1,0:T(8,128)S(1)}, bf16[288,2048]{1,0:T(8,128)(2,1)S(1)}, bf16[288,2048]{1,0:T(8,128)(2,1...) custom-call(bf16[2,288,2048]{2,1,0:T(8,128)(2,1)} %bitcast.9, ...), custom_call_target="tpu_custom_call" | custom-call | tf_op jit(solution)/shard_map/mlp_step/pallas_call | solution.py:284
  31.6 3.8 %collective-permute-start.2 = (bf16[24,896]{1,0:T(8,128)(2,1)S(1)}, bf16[24,896]{1,0:T(8,128)(2,1)S(1)}, u32[]{:S(2)}, u32[]{:S(2)}) collective-permute-start(bf16[24,896]{1,0:T(8,128)(2,1)S(1)} %get-tuple-element.25.refs_0_), channel_id=1, source_target_pairs={{0,96},{32,0},{64,32},{96,64},{1,97},{33,1},{65,33},{97,65},{2,98}... | collective-permute-start | bytes 129032 | tf_op jit(solution)/shard_map/ppermute | solution.py:321
  35.4 0.0 collective-permute-start.1
  35.4 0.7 %collective-permute-start = (bf16[24,896]{1,0:T(8,128)(2,1)S(1)}, bf16[24,896]{1,0:T(8,128)(2,1)S(1)}, u32[]{:S(2)}, u32[]{:S(2)}) collective-permute-start(bf16[24,896]{1,0:T(8,128)(2,1)S(1)} %get-tuple-element.25.refs_0_), channel_id=1, source_target_pairs={{0,32},{32,64},{64,96},{96,0},{1,33},{33,65},{65,97},{97,1},{2,34}... | collective-permute-start | bytes 129032 | tf_op jit(solution)/shard_map/ppermute | solution.py:321
  36.1 5.7 %second.1 = (bf16[2,288,2048]{2,1,0:T(8,128)(2,1)}, f32[3,288,768]{2,1,0:T(8,128)}) custom-call(bf16[288,2048]{1,0:T(8,128)(2,1)S(1)} %get-tuple-element.15.dx0, f32[3,288,768]{2,1,0:T(8,128)S(1)} %get-tuple-element.16.acc, bf16[288,2048]{1,0:T(8,128)(2,1)S(1)} %get-tuple-element.17.x1, bf16[288,2048]{1,0:T(8,128)(2,1)S(1)} %get-tuple-element.18.dy1, ...), custom_call_target="tpu_custom_call" | custom-call | flops 7000000000 | bytes 5000000 | tf_op jit(solution)/shard_map/second/pallas_call | solution.py:322
  41.8 0.0 collective-permute-done.2.refs_3_
  41.8 0.0 collective-permute-done.1.refs_2_
  41.8 0.0 collective-permute-done.refs_1_
  41.9 0.8 %last_sum.1 = f32[3,24,288]{2,1,0:T(8,128)} custom-call(bf16[24,896]{1,0:T(8,128)(2,1)S(1)} %get-tuple-element.25.refs_0_, bf16[24,896]{1,0:T(8,128)(2,1)S(1)} %collective-permute-done.refs_1_, bf16[24,896]{1,0:T(8,128)(2,1)S(1)} %collective-permute-done.1.refs_2_, bf16[24,896]{1,0:T(8,128)(2,1)S(1)} %collective-permute-done.2.refs_3_), custom_call_target="tpu_custom_call" | custom-call | tf_op jit(solution)/shard_map/last_sum/pallas_call | solution.py:336
Async XLA Ops:
  31.6 10.2 %collective-permute-start.2 = (bf16[24,896]{1,0:T(8,128)(2,1)S(1)}, bf16[24,896]{1,0:T(8,128)(2,1)S(1)}, u32[]{:S(2)}, u32[]{:S(2)}) collective-permute-start(bf16[24,896]{1,0:T(8,128)(2,1)S(1)} %get-tuple-element.25.refs_0_), channel_id=1, source_target_pairs={{0,96},{32,0},{64,32},{96,64},{1,97},{33,1},{65,33},{97,65},{2,98}... | collective-permute-start | bytes 129032 | tf_op jit(solution)/shard_map/ppermute | solution.py:321
  35.4 6.4 %collective-permute-start.1 = (bf16[24,896]{1,0:T(8,128)(2,1)S(1)}, bf16[24,896]{1,0:T(8,128)(2,1)S(1)}, u32[]{:S(2)}, u32[]{:S(2)}) collective-permute-start(bf16[24,896]{1,0:T(8,128)(2,1)S(1)} %get-tuple-element.25.refs_0_), channel_id=1, source_target_pairs={{0,64},{32,96},{64,0},{96,32},{1,65},{33,97},{65,1},{97,33},{2,66}... | collective-permute-start | bytes 129032 | tf_op jit(solution)/shard_map/ppermute | solution.py:321
  35.4 6.4 %collective-permute-start = (bf16[24,896]{1,0:T(8,128)(2,1)S(1)}, bf16[24,896]{1,0:T(8,128)(2,1)S(1)}, u32[]{:S(2)}, u32[]{:S(2)}) collective-permute-start(bf16[24,896]{1,0:T(8,128)(2,1)S(1)} %get-tuple-element.25.refs_0_), channel_id=1, source_target_pairs={{0,32},{32,64},{64,96},{96,0},{1,33},{33,65},{65,97},{97,1},{2,34}... | collective-permute-start | bytes 129032 | tf_op jit(solution)/shard_map/ppermute | solution.py:321

commit v5 on v4

--- a/solution.py
+++ b/solution.py
@@ -19,10 +19,10 @@
 
 def kernel(n_dp, n_row, n_x, micro, tokens, d_model, ff, blk,
            x_hbm, dy_hbm, w1_hbm, w3_hbm, w2_hbm, g_hbm,
-           dx0, acc, x1, dy1, h1, da1, db1, w1, w3, r,
-           x0, dy0, h0, da0, db0, g_v, shard, wbuf, g1, g3, g2,
-           gt, pr, part, rx1, rx0, mid, rx2, q, ry,
-           load_sem, g_sem, ag_s, ag_r, rs_s, rs_r):
+           dx0, dx1, acc, gn, dy1, h1,
+           x0, x1, dy0, h0, da0, da1, db0, db1, w1, w3, g_v, shard, wbuf, g1, g3, g2,
+           gt, pr, part, rx1, rx0, mid, rx2, q, ry, r, rz,
+           load_sem, g_sem, ag_s, ag_r, rs_s, rs_r, dp_ready):
     z, y, f = lax.axis_index("dp"), lax.axis_index("row"), lax.axis_index("fsdp")
     x, c = f // 2, f % 2
     main, tail = 256, d_model - 256
@@ -42,6 +42,11 @@
     barrier = pltpu.get_barrier_semaphore()
     for peer in peers:
         pl.semaphore_signal(barrier, inc=1, device_id=peer, device_id_type=MESH)
+
+    for d in range(1, n_dp):
+        @pl.when(z + d < n_dp)
+        def _():
+            pl.semaphore_signal(barrier, inc=1, device_id=(z + d, y, f), device_id_type=MESH)
 
     g_loads = [pltpu.make_async_copy(g_hbm.at[s], g_v.at[s], g_sem.at[s]) for s in range(3)]
     t_loads = [[pltpu.make_async_copy(src.at[m], dst[m], load_sem.at[3 + 2 * m + i])
@@ -59,7 +64,11 @@
     tails = [s[:, main:].astype(F32) for s in (s1, s3, s2)] + [jnp.zeros((blk, 128 - 3 * tail), F32)]
     wbuf[y, x, c, :, 3 * main:] = jnp.concatenate(tails, axis=1).astype(BF16)
 
-    pl.semaphore_wait(barrier, len(peers))
+    pl.semaphore_wait(barrier, len(peers) + z)
+    for d in range(1, n_dp):
+        @pl.when(z >= d)
+        def _():
+            pl.semaphore_signal(dp_ready, inc=1, device_id=(z - d, y, f), device_id_type=MESH)
 
     sent = []
     count = {"ag": 0, "rs": 0}
@@ -182,16 +191,15 @@
     take(2, -1)
     take(-1, 2)
     take(1, 2)
-    u0 = [send("rs", part.at[up, hi], rx0.at[0], device(1, 0)),
-          send("rs", part.at[um, lo], rx0.at[1], device(-1, 0))]
-    ahead(mids, 1)
-
     for copy in u1:
         copy.wait_recv()
     half = side // 2
     mid[0] = (part[up, :half].astype(F32) + rx1[0].astype(F32)).astype(BF16)
     mid[1] = (part[um, half:].astype(F32) + rx1[1].astype(F32)).astype(BF16)
     u2 = [send("rs", mid.at[0], rx2.at[0], device(1, 0)), send("rs", mid.at[1], rx2.at[1], device(-1, 0))]
+    u0 = [send("rs", part.at[up, hi], rx0.at[0], device(1, 0)),
+          send("rs", part.at[um, lo], rx0.at[1], device(-1, 0))]
+    ahead(mids, 1)
 
     far = [(2, 1), (2, -1), (-1, 2), (1, 2)]
     for key in far:
@@ -199,15 +207,14 @@
     fill(far)
     ahead(far, 0)
     take(2, 2)
-    ahead(far, 1)
-    pairs[2, 2].wait_recv()
-    fill([(2, 2)])
-
     for copy in u0 + u2:
         copy.wait_recv()
     q[:half] = (part[u, :half].astype(F32) + rx2[0].astype(F32) + rx0[1].astype(F32)).astype(BF16)
     q[half:] = (part[u, half:].astype(F32) + rx2[1].astype(F32) + rx0[0].astype(F32)).astype(BF16)
     vs = [send("rs", q.at[(v + d) % side], ry.at[d - 1], device(0, d)) for d in (2, 1, 3)]
+    ahead(far, 1)
+    pairs[2, 2].wait_recv()
+    fill([(2, 2)])
 
     def across(lo, hi):
         return wbuf[..., lo:hi].astype(F32).reshape(ff, hi - lo).astype(BF16).T
@@ -218,48 +225,52 @@
     w1[main:, :] = ends[:tail]
     w3[main:, :] = ends[tail:2 * tail]
 
-    ahead([(2, 2)], 0)
-    dx0[...] = (mm(w1[...], da0[...]) + mm(w3[...], db0[...])).astype(BF16)
-    acc[0] = mm(x0[...], da0[...], NT)
-    acc[1] = mm(x0[...], db0[...], NT)
-    acc[2] = mm(dy0[...], h0[...], NT)
-    ahead([(2, 2)], 1)
-    for copy in vs:
+    cut = tokens // 2
+    for m, (x_m, dy_m, h_m, da_m, db_m, dx_m) in enumerate(((x0, dy0, h0, da0, db0, dx0), (x1, dy1, h1, da1, db1, dx1))):
+        ahead([(2, 2)], m)
+        for lo, hi in ((0, cut), (cut, tokens)) if m == 0 else ((0, tokens),):
+            da, db = da_m[:, lo:hi], db_m[:, lo:hi]
+            dx_m[:, lo:hi] = (mm(w1[...], da) + mm(w3[...], db)).astype(BF16)
+            first = m == 0 and lo == 0
+            acc[0] = (0 if first else acc[0]) + mm(x_m[:, lo:hi], da, NT)
+            acc[1] = (0 if first else acc[1]) + mm(x_m[:, lo:hi], db, NT)
+            if m == 0:
+                acc[2] = (0 if first else acc[2]) + mm(dy_m[:, lo:hi], h_m[:, lo:hi], NT)
+            if first:
+                for copy in vs:
+                    copy.wait_recv()
+                own = q[v].astype(F32)
+                for d in range(1, side):
+                    own += ry[d - 1].astype(F32)
+                r[...] = own.astype(BF16)
+
+                @pl.when(z < n_dp - 1)
+                def _():
+                    pl.semaphore_wait(dp_ready, n_dp - 1 - z)
+
+                zs = [send("rs", r, rz.at[z], ((z + d) % n_dp, y, f)) for d in (2, 1, 3)]
+                rz[z] = r[...]
+    for copy in zs:
         copy.wait_recv()
-    own = q[v].astype(F32)
-    for d in range(1, side):
-        own += ry[d - 1].astype(F32)
-    r[...] = own.astype(BF16)
-    for copy in sent:
-        copy.wait_send()
-
-
-def second(dx0, acc, x1, dy1, h1, da1, db1, w1, w3, dx_hbm, dw_hbm, dx1, dw, sems):
-    outs = [pltpu.make_async_copy(dx0, dx_hbm.at[0], sems.at[0]), pltpu.make_async_copy(dx1, dx_hbm.at[1], sems.at[1])]
-    outs += [pltpu.make_async_copy(dw.at[s], dw_hbm.at[s], sems.at[2 + s]) for s in range(3)]
-    outs[0].start()
-    dw[0] = acc[0] + mm(x1[...], da1[...], NT)
-    dw[1] = acc[1] + mm(x1[...], db1[...], NT)
-    dx1[...] = (mm(w1[...], da1[...]) + mm(w3[...], db1[...])).astype(BF16)
-    for i in (2, 3, 1):
-        outs[i].start()
-    dw[2] = acc[2] + mm(dy1[...], h1[...], NT)
-    outs[4].start()
-    for out in outs:
-        out.wait()
-
-
-def last(n_dp, main, tail, *refs):
-    parts, gn, stack = refs[:n_dp], refs[n_dp], refs[n_dp + 1]
-    z = lax.axis_index("dp")
-    for d in range(n_dp):
-        stack[(z + n_dp - d) % n_dp] = parts[d][...]
-    total = stack[0].astype(F32)
+    total = rz[0].astype(F32)
     for d in range(1, n_dp):
-        total += stack[d].astype(F32)
+        total += rz[d].astype(F32)
     for s in range(3):
         gn[s, :, :main] = total[:, s * main:(s + 1) * main]
         gn[s, :, main:] = total[:, 3 * main + s * tail:3 * main + (s + 1) * tail]
+    for copy in sent:
+        copy.wait_send()
+
+
+def second(dx0, dx1, acc, gn, dy1, h1, dx_hbm, gn_hbm, dw_hbm, dw, sems):
+    moves = [(dx0, dx_hbm.at[0]), (dx1, dx_hbm.at[1]), (acc.at[0], dw_hbm.at[0]), (acc.at[1], dw_hbm.at[1]), (gn, gn_hbm), (dw, dw_hbm.at[2])]
+    outs = [pltpu.make_async_copy(src, dst, sems.at[i]) for i, (src, dst) in enumerate(moves)]
+    for out in outs[:-1]:
+        out.start()
+    dw[...] = acc[2] + mm(dy1[...], h1[...], NT)
+    outs[-1].start()
+    for out in outs:
+        out.wait()
 
 
 def solution(mesh):
@@ -279,19 +290,17 @@
         args = [x_dev.transpose(0, 2, 1), dy_dev.transpose(0, 2, 1), gate.T, up_w.T, down, g_dev[0]]
         args = [pltpu.with_memory_space_constraint(arg, pltpu.HBM) for arg in args]
         half, mids = (d_model, tokens), (ff, tokens)
-        outs = [pltpu.VMEM(half, BF16), pltpu.VMEM((3, d_model, ff), F32)] + [pltpu.VMEM(half, BF16)] * 2
-        outs += [pltpu.VMEM(mids, BF16)] * 3 + [pltpu.VMEM((d_model, ff), BF16)] * 2 + [pltpu.VMEM((blk, wide), BF16)]
-        *rest, r = pl.pallas_call(
+        outs = [pltpu.VMEM(half, BF16)] * 2 + [pltpu.VMEM((3, d_model, ff), F32), pltpu.VMEM((3, blk, d_model), F32)]
+        outs += [pltpu.VMEM(half, BF16), pltpu.VMEM(mids, BF16)]
+        parts = pl.pallas_call(
             body,
             in_specs=[hbm] * 6,
             out_specs=[vmem] * len(outs),
             out_shape=outs,
             scratch_shapes=[
-                pltpu.VMEM(half, BF16),
-                pltpu.VMEM(half, BF16),
-                pltpu.VMEM(mids, BF16),
-                pltpu.VMEM(mids, BF16),
-                pltpu.VMEM(mids, BF16),
+                *[pltpu.VMEM(half, BF16)] * 3,
+                *[pltpu.VMEM(mids, BF16)] * 5,
+                *[pltpu.VMEM((d_model, ff), BF16)] * 2,
                 pltpu.VMEM((3, d_model, ff), F32),
                 pltpu.VMEM((3, blk, d_model), BF16),
                 pltpu.VMEM((n_row, n_x, 2, blk, wide), BF16),
@@ -307,41 +316,30 @@
                 pltpu.VMEM((2, 2, blk, wide), BF16),
                 pltpu.VMEM((4, blk, wide), BF16),
                 pltpu.VMEM((3, blk, wide), BF16),
+                pltpu.VMEM((blk, wide), BF16),
+                pltpu.VMEM((n_dp, blk, wide), BF16),
                 pltpu.SemaphoreType.DMA((3 + 2 * micro,)),
                 pltpu.SemaphoreType.DMA((3,)),
                 pltpu.SemaphoreType.DMA((31,)),
                 pltpu.SemaphoreType.DMA((31,)),
-                pltpu.SemaphoreType.DMA((10,)),
-                pltpu.SemaphoreType.DMA((10,)),
+                pltpu.SemaphoreType.DMA((13,)),
+                pltpu.SemaphoreType.DMA((13,)),
+                pltpu.SemaphoreType.REGULAR,
             ],
             compiler_params=pltpu.CompilerParams(
-                collective_id=0, has_side_effects=True, vmem_limit_bytes=34 * 2**20),
+                collective_id=0, has_side_effects=True, vmem_limit_bytes=44 * 2**20),
             name="mlp_step",
         )(*args)
-        ring = [r] + [lax.ppermute(r, "dp", [(i, (i + d) % n_dp) for i in range(n_dp)]) for d in range(1, n_dp)]
-        dx_t, dw = pl.pallas_call(
+        dx_t, gn, dw = pl.pallas_call(
             second,
-            in_specs=[vmem] * len(rest),
-            out_specs=[hbm] * 2,
-            out_shape=[jax.ShapeDtypeStruct((micro, d_model, tokens), BF16), jax.ShapeDtypeStruct((3, d_model, ff), F32)],
-            scratch_shapes=[pltpu.VMEM(half, BF16), pltpu.VMEM((3, d_model, ff), F32), pltpu.SemaphoreType.DMA((5,))],
-            compiler_params=pltpu.CompilerParams(vmem_limit_bytes=16 * 2**20),
-            cost_estimate=pl.CostEstimate(flops=7 * 10**9, bytes_accessed=5 * 10**6, transcendentals=0),
+            in_specs=[vmem] * len(parts),
+            out_specs=[hbm] * 3,
+            out_shape=[jax.ShapeDtypeStruct(shape, dtype) for shape, dtype in
+                       (((micro, d_model, tokens), BF16), ((3, blk, d_model), F32), ((3, d_model, ff), F32))],
+            scratch_shapes=[pltpu.VMEM((d_model, ff), F32), pltpu.SemaphoreType.DMA((6,))],
+            compiler_params=pltpu.CompilerParams(vmem_limit_bytes=12 * 2**20),
             name="second",
-        )(*rest)
-
-        def finish(*refs):
-            last(n_dp, 256, d_model - 256, *refs)
-
-        gn = pl.pallas_call(
-            finish,
-            in_specs=[vmem] * n_dp,
-            out_specs=vmem,
-            out_shape=jax.ShapeDtypeStruct((3, blk, d_model), F32),
-            scratch_shapes=[pltpu.VMEM((n_dp, blk, wide), BF16)],
-            compiler_params=pltpu.CompilerParams(vmem_limit_bytes=4 * 2**20),
-            name="last_sum",
-        )(*ring)
+        )(*parts)
         return dx_t.transpose(0, 2, 1), gn.transpose(0, 2, 1), dw[None]
 
     in_specs = (P(None, TOK_AXES, None), P(None, TOK_AXES, None), P(None, GROUP_AXES), P(None, GROUP_AXES), P(GROUP_AXES, None), P(TOK_AXES, None, None, None))

time: 42.9 us -> 39.9 us (0.930)
  starting transfers between devices: 4.51 us -> 0 us
  Pallas kernels: 37.4 us -> 39 us
    pallas_call x1, Pallas kernels: 30.9 us -> 36.6 us  [local_step(): pl.pallas_call(body, in_specs=[hbm] * 6, out_specs=[vmem] * len(outs), ou...]
    ppermute x3 -> x0, starting transfers between devices: 4.51 us -> none  [local_step(): lax.ppermute(r, 'dp', [(i, (i + d) % n_dp) for i in range(n_dp)])]
    pallas_call x2 -> x1, Pallas kernels: 6.48 us -> 2.36 us  [local_step(): pl.pallas_call(second, in_specs=[vmem] * len(parts), out_specs=[hbm] * 3,...]
  transfers between devices with their start and end apart: 3 -> 0, of which waited for: 0 -> 0; matrix products, arithmetic and copies ran while one was open for 0% -> 0% of each run, Pallas kernels for 13% -> 0%
where the time goes in v5:
time: 39.9 us; the launch traced here: 39.8 us
  Pallas kernels  39 us (98%)
  between operations  0.8 us (2%)
    pallas_call x1, Pallas kernels, local_step(): pl.pallas_call(body, in_specs=[hbm] * 6, out_specs=[vmem] * len(outs), ou...  36.6 us
    pallas_call x1, Pallas kernels, local_step(): pl.pallas_call(second, in_specs=[vmem] * len(parts), out_specs=[hbm] * 3,...  2.36 us

profile of v5, /device:TPU:1, one launch (start us, length us, event | category | flops | bytes accessed | tf_op | source)
XLA Modules:
  0.0 39.8 jit_solution(9336121759667993339)
XLA Ops:
  0.6 36.6 %mlp_step.1 = (bf16[288,2048]{1,0:T(8,128)(2,1)S(1)}, bf16[288,2048]{1,0:T(8,128)(2,1)S(1)}, f32[3,288,768]{2,1,0:T(8,128)S(1)}, f32[3,24,288]{2,1,0:T(8,128)S(1...) custom-call(bf16[2,288,2048]{2,1,0:T(8,128)(2,1)} %bitcast.9, bf16[2,288,2048]{2,1,0:T(8,128)(2,1)} %bitcast.10, ...), custom_call_target="tpu_custom_call" | custom-call | tf_op jit(solution)/shard_map/mlp_step/pallas_call | solution.py:295
  37.3 2.4 %second.1 = (bf16[2,288,2048]{2,1,0:T(8,128)(2,1)}, f32[3,24,288]{2,1,0:T(8,128)}, f32[3,288,768]{2,1,0:T(8,128)}) custom-call(bf16[288,2048]{1,0:T(8,128)(2,1)S(1)} %get-tuple-element.12.dx0, bf16[288,2048]{1,0:T(8,128)(2,1)S(1)} %get-tuple-element.13.dx1, f32[3,288,768]{2,1,0:T(8,128)S(1)} %get-tuple-element.14.acc, ...), custom_call_target="tpu_custom_call" | custom-call | tf_op jit(solution)/shard_map/second/pallas_call | solution.py:333

commit v6 on v5

--- a/solution.py
+++ b/solution.py
@@ -19,10 +19,10 @@
 
 def kernel(n_dp, n_row, n_x, micro, tokens, d_model, ff, blk,
            x_hbm, dy_hbm, w1_hbm, w3_hbm, w2_hbm, g_hbm,
-           dx0, dx1, acc, gn, dy1, h1,
-           x0, x1, dy0, h0, da0, da1, db0, db1, w1, w3, g_v, shard, wbuf, g1, g3, g2,
+           dx0, dx1, acc, gn, x1, dy1, h1, da1, db1,
+           x0, dy0, h0, da0, db0, w1, w3, g_v, shard, wbuf, g1, g3, g2,
            gt, pr, part, rx1, rx0, mid, rx2, q, ry, r, rz,
-           load_sem, g_sem, ag_s, ag_r, rs_s, rs_r, dp_ready):
+           load_sem, g_sem, ag_s, ag_r, rs_s, rs_r, dp_ready, ready):
     z, y, f = lax.axis_index("dp"), lax.axis_index("row"), lax.axis_index("fsdp")
     x, c = f // 2, f % 2
     main, tail = 256, d_model - 256
@@ -37,11 +37,22 @@
         return (z, yy, xx * 2 + c)
 
     partner = (z, y, x * 2 + 1 - c)
-    peers = [partner, device(1, 0), device(-1, 0), device(0, 1), device(0, -1), device(0, 2), device(2, 0)]
+    rank = y * 2 * n_x + f
+    near_by = [(1, 0), (-1, 0), (0, 1), (0, -1), (2, 0), (0, 2)]
+    peers = [(device(du, dv), k) for k, (du, dv) in enumerate(near_by)] + [(partner, 6)]
+    back_to = [1, 0, 3, 2, 4, 5, 6]
+
+    def rank_of(peer):
+        return peer[1] * 2 * n_x + peer[2]
 
     barrier = pltpu.get_barrier_semaphore()
-    for peer in peers:
-        pl.semaphore_signal(barrier, inc=1, device_id=peer, device_id_type=MESH)
+    lower = z
+    for peer, k in peers:
+        lower += (rank_of(peer) < rank).astype(jnp.int32)
+
+        @pl.when(rank_of(peer) > rank)
+        def _():
+            pl.semaphore_signal(barrier, inc=1, device_id=peer, device_id_type=MESH)
 
     for d in range(1, n_dp):
         @pl.when(z + d < n_dp)
@@ -64,7 +75,15 @@
     tails = [s[:, main:].astype(F32) for s in (s1, s3, s2)] + [jnp.zeros((blk, 128 - 3 * tail), F32)]
     wbuf[y, x, c, :, 3 * main:] = jnp.concatenate(tails, axis=1).astype(BF16)
 
-    pl.semaphore_wait(barrier, len(peers) + z)
+    @pl.when(lower > 0)
+    def _():
+        pl.semaphore_wait(barrier, lower)
+
+    for peer, k in peers:
+        @pl.when(rank_of(peer) < rank)
+        def _():
+            pl.semaphore_signal(ready.at[back_to[k]], inc=1, device_id=peer, device_id_type=MESH)
+
     for d in range(1, n_dp):
         @pl.when(z >= d)
         def _():
@@ -73,14 +92,15 @@
     sent = []
     count = {"ag": 0, "rs": 0}
 
-    def send(kind, src, dst, where):
+    def send(kind, src, dst, where, start=True):
         i = count[kind]
         count[kind] += 1
         ss, rr = (ag_s, ag_r) if kind == "ag" else (rs_s, rs_r)
         copy = pltpu.make_async_remote_copy(
             src_ref=src, dst_ref=dst, send_sem=ss.at[i], recv_sem=rr.at[i],
             device_id=where, device_id_type=MESH)
-        copy.start()
+        if start:
+            copy.start()
         sent.append(copy)
         return copy
 
@@ -101,9 +121,23 @@
             forward(du, dv, su, sv)
         share(du, dv)
 
-    for su, sv in ((1, 0), (-1, 0), (0, 1), (0, -1), (2, 0)):
-        forward(0, 0, su, sv)
-    share(0, 0)
+    own_block = wbuf.at[y, x, c]
+    firsts = {}
+    for k in (0, 1, 2, 3, 6, 4):
+        firsts[k] = send("ag", own_block, own_block, peers[k][0], start=False)
+    arrive.update({(-1, 0): firsts[0], (1, 0): firsts[1], (0, -1): firsts[2], (0, 1): firsts[3], (2, 0): firsts[4]})
+    pairs[0, 0] = firsts[6]
+
+    for k, copy in firsts.items():
+        @pl.when(rank_of(peers[k][0]) < rank)
+        def _():
+            copy.start()
+
+    for k, copy in firsts.items():
+        @pl.when(rank_of(peers[k][0]) > rank)
+        def _():
+            pl.semaphore_wait(ready.at[k], 1)
+            copy.start()
 
     def turn(s):
         g_loads[s].wait()
@@ -140,15 +174,16 @@
             for ref, value in zip(((h0, da0, db0), (h1, da1, db1))[m], (h, da, db)):
                 ref[to, lo:hi] = value[at]
 
+    turn(0)
+    turn(1)
+    turn(2)
+    turn_tail()
+    pair = send("rs", gt.at[:, :, 1 - c], pr, partner)
     for load in t_loads[0]:
         load.wait()
     pairs[0, 0].wait_recv()
     fill([(0, 0)])
     ahead([(0, 0)], 0)
-    turn(0)
-    turn(1)
-    turn(2)
-    turn_tail()
 
     take(-1, 0, (0, 1), (0, -1))
     take(1, 0, (0, 1), (0, -1))
@@ -157,14 +192,6 @@
     for load in t_loads[1]:
         load.wait()
     ahead([(0, 0)], 1)
-    near = [(-1, 0), (1, 0), (0, -1), (0, 1)]
-    take(2, 0, (0, 1), (0, -1))
-    for key in near:
-        pairs[key].wait_recv()
-    pair = send("rs", gt.at[:, :, 1 - c], pr, partner)
-    fill(near)
-    ahead(near, 0)
-    ahead(near, 1, 0, tokens // 2)
     pair.wait_recv()
     for yy in range(n_row):
         for xx in range(n_x):
@@ -173,48 +200,57 @@
     u, v = x * (1 - c) + y * c, y * (1 - c) + x * c
     um, up, uo = (u + side - 1) % side, (u + 1) % side, (u + 2) % side
     lo, hi = pl.ds(0, side // 2), pl.ds(side // 2, side // 2)
-
+    near = [(-1, 0), (1, 0), (0, -1), (0, 1)]
+    take(2, 0, (0, 1), (0, -1))
+    u1 = [send("rs", part.at[uo, lo], rx1.at[0], device(1, 0)),
+          send("rs", part.at[uo, hi], rx1.at[1], device(-1, 0))]
+    for key in near:
+        pairs[key].wait_recv()
+    fill(near)
+    ahead(near, 0)
+    ahead(near, 1, 0, tokens // 2)
     take(-1, -1, (0, 1))
     take(1, 1, (0, -1))
     take(-1, 1)
     take(1, -1)
     take(0, 2)
-    u1 = [send("rs", part.at[uo, lo], rx1.at[0], device(1, 0)),
-          send("rs", part.at[uo, hi], rx1.at[1], device(-1, 0))]
+    u0 = [send("rs", part.at[up, hi], rx0.at[0], device(1, 0)),
+          send("rs", part.at[um, lo], rx0.at[1], device(-1, 0))]
     ahead(near, 1, tokens // 2)
-    mids = [(2, 0), (0, 2), (-1, -1), (1, 1), (-1, 1), (1, -1)]
-    for key in mids:
-        pairs[key].wait_recv()
-    fill(mids)
-    ahead(mids, 0)
     take(2, 1, (0, -1))
     take(2, -1)
-    take(-1, 2)
-    take(1, 2)
+    mids = [(2, 0), (0, 2), (-1, -1), (1, 1), (-1, 1), (1, -1)]
     for copy in u1:
         copy.wait_recv()
     half = side // 2
     mid[0] = (part[up, :half].astype(F32) + rx1[0].astype(F32)).astype(BF16)
     mid[1] = (part[um, half:].astype(F32) + rx1[1].astype(F32)).astype(BF16)
     u2 = [send("rs", mid.at[0], rx2.at[0], device(1, 0)), send("rs", mid.at[1], rx2.at[1], device(-1, 0))]
-    u0 = [send("rs", part.at[up, hi], rx0.at[0], device(1, 0)),
-          send("rs", part.at[um, lo], rx0.at[1], device(-1, 0))]
+    for key in mids:
+        pairs[key].wait_recv()
+    fill(mids)
+    ahead(mids, 0, 0, tokens * 3 // 4)
+    take(-1, 2)
+    take(1, 2)
+    take(2, 2)
+    ahead(mids, 0, tokens * 3 // 4)
     ahead(mids, 1)
 
-    far = [(2, 1), (2, -1), (-1, 2), (1, 2)]
+    far = [(2, 1), (2, -1), (-1, 2), (1, 2), (2, 2)]
     for key in far:
         pairs[key].wait_recv()
-    fill(far)
-    ahead(far, 0)
-    take(2, 2)
     for copy in u0 + u2:
         copy.wait_recv()
     q[:half] = (part[u, :half].astype(F32) + rx2[0].astype(F32) + rx0[1].astype(F32)).astype(BF16)
     q[half:] = (part[u, half:].astype(F32) + rx2[1].astype(F32) + rx0[0].astype(F32)).astype(BF16)
+
+    @pl.when(rank_of(peers[5][0]) > rank)
+    def _():
+        pl.semaphore_wait(ready.at[5], 1)
+
     vs = [send("rs", q.at[(v + d) % side], ry.at[d - 1], device(0, d)) for d in (2, 1, 3)]
-    ahead(far, 1)
-    pairs[2, 2].wait_recv()
-    fill([(2, 2)])
+    fill(far)
+    ahead(far, 0)
 
     def across(lo, hi):
         return wbuf[..., lo:hi].astype(F32).reshape(ff, hi - lo).astype(BF16).T
@@ -224,32 +260,26 @@
     ends = across(3 * main, 3 * main + 128)
     w1[main:, :] = ends[:tail]
     w3[main:, :] = ends[tail:2 * tail]
-
-    cut = tokens // 2
-    for m, (x_m, dy_m, h_m, da_m, db_m, dx_m) in enumerate(((x0, dy0, h0, da0, db0, dx0), (x1, dy1, h1, da1, db1, dx1))):
-        ahead([(2, 2)], m)
-        for lo, hi in ((0, cut), (cut, tokens)) if m == 0 else ((0, tokens),):
-            da, db = da_m[:, lo:hi], db_m[:, lo:hi]
-            dx_m[:, lo:hi] = (mm(w1[...], da) + mm(w3[...], db)).astype(BF16)
-            first = m == 0 and lo == 0
-            acc[0] = (0 if first else acc[0]) + mm(x_m[:, lo:hi], da, NT)
-            acc[1] = (0 if first else acc[1]) + mm(x_m[:, lo:hi], db, NT)
-            if m == 0:
-                acc[2] = (0 if first else acc[2]) + mm(dy_m[:, lo:hi], h_m[:, lo:hi], NT)
-            if first:
-                for copy in vs:
-                    copy.wait_recv()
-                own = q[v].astype(F32)
-                for d in range(1, side):
-                    own += ry[d - 1].astype(F32)
-                r[...] = own.astype(BF16)
-
-                @pl.when(z < n_dp - 1)
-                def _():
-                    pl.semaphore_wait(dp_ready, n_dp - 1 - z)
-
-                zs = [send("rs", r, rz.at[z], ((z + d) % n_dp, y, f)) for d in (2, 1, 3)]
-                rz[z] = r[...]
+    ahead(far, 1)
+
+    for copy in vs:
+        copy.wait_recv()
+    own = q[v].astype(F32)
+    for d in range(1, side):
+        own += ry[d - 1].astype(F32)
+    r[...] = own.astype(BF16)
+
+    @pl.when(z < n_dp - 1)
+    def _():
+        pl.semaphore_wait(dp_ready, n_dp - 1 - z)
+
+    zs = [send("rs", r, rz.at[z], ((z + d) % n_dp, y, f)) for d in (2, 1, 3)]
+    rz[z] = r[...]
+    dx0[...] = (mm(w1[...], da0[...]) + mm(w3[...], db0[...])).astype(BF16)
+    acc[0] = mm(x0[...], da0[...], NT)
+    acc[1] = mm(x0[...], db0[...], NT)
+    acc[2] = mm(dy0[...], h0[...], NT)
+    dx1[...] = (mm(w1[...], da1[...]) + mm(w3[...], db1[...])).astype(BF16)
     for copy in zs:
         copy.wait_recv()
     total = rz[0].astype(F32)
@@ -262,13 +292,14 @@
         copy.wait_send()
 
 
-def second(dx0, dx1, acc, gn, dy1, h1, dx_hbm, gn_hbm, dw_hbm, dw, sems):
-    moves = [(dx0, dx_hbm.at[0]), (dx1, dx_hbm.at[1]), (acc.at[0], dw_hbm.at[0]), (acc.at[1], dw_hbm.at[1]), (gn, gn_hbm), (dw, dw_hbm.at[2])]
+def second(dx0, dx1, acc, gn, x1, dy1, h1, da1, db1, dx_hbm, gn_hbm, dw_hbm, dw, sems):
+    moves = [(dx0, dx_hbm.at[0]), (dx1, dx_hbm.at[1]), (gn, gn_hbm)] + [(dw.at[s], dw_hbm.at[s]) for s in range(3)]
     outs = [pltpu.make_async_copy(src, dst, sems.at[i]) for i, (src, dst) in enumerate(moves)]
-    for out in outs[:-1]:
+    for out in outs[:3]:
         out.start()
-    dw[...] = acc[2] + mm(dy1[...], h1[...], NT)
-    outs[-1].start()
+    for s, (lhs, rhs) in enumerate(((x1, da1), (x1, db1), (dy1, h1))):
+        dw[s] = acc[s] + mm(lhs[...], rhs[...], NT)
+        outs[3 + s].start()
     for out in outs:
         out.wait()
 
@@ -291,15 +322,15 @@
         args = [pltpu.with_memory_space_constraint(arg, pltpu.HBM) for arg in args]
         half, mids = (d_model, tokens), (ff, tokens)
         outs = [pltpu.VMEM(half, BF16)] * 2 + [pltpu.VMEM((3, d_model, ff), F32), pltpu.VMEM((3, blk, d_model), F32)]
-        outs += [pltpu.VMEM(half, BF16), pltpu.VMEM(mids, BF16)]
+        outs += [pltpu.VMEM(half, BF16)] * 2 + [pltpu.VMEM(mids, BF16)] * 3
         parts = pl.pallas_call(
             body,
             in_specs=[hbm] * 6,
             out_specs=[vmem] * len(outs),
             out_shape=outs,
             scratch_shapes=[
-                *[pltpu.VMEM(half, BF16)] * 3,
-                *[pltpu.VMEM(mids, BF16)] * 5,
+                *[pltpu.VMEM(half, BF16)] * 2,
+                *[pltpu.VMEM(mids, BF16)] * 3,
                 *[pltpu.VMEM((d_model, ff), BF16)] * 2,
                 pltpu.VMEM((3, d_model, ff), F32),
                 pltpu.VMEM((3, blk, d_model), BF16),
@@ -325,9 +356,10 @@
                 pltpu.SemaphoreType.DMA((13,)),
                 pltpu.SemaphoreType.DMA((13,)),
                 pltpu.SemaphoreType.REGULAR,
+                pltpu.SemaphoreType.REGULAR((7,)),
             ],
             compiler_params=pltpu.CompilerParams(
-                collective_id=0, has_side_effects=True, vmem_limit_bytes=44 * 2**20),
+                collective_id=0, has_side_effects=True, vmem_limit_bytes=38 * 2**20),
             name="mlp_step",
         )(*args)
         dx_t, gn, dw = pl.pallas_call(
@@ -336,7 +368,7 @@
             out_specs=[hbm] * 3,
             out_shape=[jax.ShapeDtypeStruct(shape, dtype) for shape, dtype in
                        (((micro, d_model, tokens), BF16), ((3, blk, d_model), F32), ((3, d_model, ff), F32))],
-            scratch_shapes=[pltpu.VMEM((d_model, ff), F32), pltpu.SemaphoreType.DMA((6,))],
+            scratch_shapes=[pltpu.VMEM((3, d_model, ff), F32), pltpu.SemaphoreType.DMA((6,))],
             compiler_params=pltpu.CompilerParams(vmem_limit_bytes=12 * 2**20),
             name="second",
         )(*parts)

time: 39.9 us -> 38.5 us (0.965)
  Pallas kernels: 39 us -> 37.6 us
    pallas_call x1, Pallas kernels: 36.6 us -> 33.6 us  [local_step(): pl.pallas_call(body, in_specs=[hbm] * 6, out_specs=[vmem] * len(outs), ou...]
    pallas_call x1, Pallas kernels: 2.36 us -> 3.98 us  [local_step(): pl.pallas_call(second, in_specs=[vmem] * len(parts), out_specs=[hbm] * 3,...]
where the time goes in v6:
time: 38.5 us; the launch traced here: 38.4 us
  Pallas kernels  37.6 us (98%)
  between operations  0.8 us (2%)
    pallas_call x1, Pallas kernels, local_step(): pl.pallas_call(body, in_specs=[hbm] * 6, out_specs=[vmem] * len(outs), ou...  33.6 us
    pallas_call x1, Pallas kernels, local_step(): pl.pallas_call(second, in_specs=[vmem] * len(parts), out_specs=[hbm] * 3,...  3.98 us

profile of v6, /device:TPU:1, one launch (start us, length us, event | category | flops | bytes accessed | tf_op | source)
XLA Modules:
  0.0 38.4 jit_solution(8313637761390871674)
XLA Ops:
  0.6 33.6 %mlp_step.1 = (bf16[288,2048]{1,0:T(8,128)(2,1)S(1)}, bf16[288,2048]{1,0:T(8,128)(2,1)S(1)}, f32[3,288,768]{2,1,0:T(8,128)S(1)}, f32[3,24,288]{2,1,0:T(8,128)S(1...) custom-call(bf16[2,288,2048]{2,1,0:T(8,128)(2,1)} %bitcast.9, ...), custom_call_target="tpu_custom_call" | custom-call | tf_op jit(solution)/shard_map/mlp_step/pallas_call | solution.py:326
  34.3 4.0 %second.1 = (bf16[2,288,2048]{2,1,0:T(8,128)(2,1)}, f32[3,24,288]{2,1,0:T(8,128)}, f32[3,288,768]{2,1,0:T(8,128)}) custom-call(bf16[288,2048]{1,0:T(8,128)(2,1)S(1)} %get-tuple-element.15.dx0, bf16[288,2048]{1,0:T(8,128)(2,1)S(1)} %get-tuple-element.16.dx1, f32[3,288,768]{2,1,0:T(8,128)S(1)} %get-tuple-element.17.acc, ...), custom_call_target="tpu_custom_call" | custom-call | tf_op jit(solution)/shard_map/second/pallas_call | solution.py:365

commit v7 on v6

--- a/solution.py
+++ b/solution.py
@@ -123,9 +123,9 @@
 
     own_block = wbuf.at[y, x, c]
     firsts = {}
-    for k in (0, 1, 2, 3, 6, 4):
+    for k in (0, 1, 2, 3, 6, 4, 5):
         firsts[k] = send("ag", own_block, own_block, peers[k][0], start=False)
-    arrive.update({(-1, 0): firsts[0], (1, 0): firsts[1], (0, -1): firsts[2], (0, 1): firsts[3], (2, 0): firsts[4]})
+    arrive.update({(-1, 0): firsts[0], (1, 0): firsts[1], (0, -1): firsts[2], (0, 1): firsts[3], (2, 0): firsts[4], (0, 2): firsts[5]})
     pairs[0, 0] = firsts[6]
 
     for k, copy in firsts.items():
@@ -187,8 +187,10 @@
 
     take(-1, 0, (0, 1), (0, -1))
     take(1, 0, (0, 1), (0, -1))
-    take(0, 1, (0, -1))
+    take(0, 1)
     take(0, -1)
+    take(2, 0, (0, 1), (0, -1))
+    take(0, 2)
     for load in t_loads[1]:
         load.wait()
     ahead([(0, 0)], 1)
@@ -200,26 +202,23 @@
     u, v = x * (1 - c) + y * c, y * (1 - c) + x * c
     um, up, uo = (u + side - 1) % side, (u + 1) % side, (u + 2) % side
     lo, hi = pl.ds(0, side // 2), pl.ds(side // 2, side // 2)
-    near = [(-1, 0), (1, 0), (0, -1), (0, 1)]
-    take(2, 0, (0, 1), (0, -1))
+    near = [(-1, 0), (1, 0), (0, -1), (0, 1), (2, 0), (0, 2)]
     u1 = [send("rs", part.at[uo, lo], rx1.at[0], device(1, 0)),
           send("rs", part.at[uo, hi], rx1.at[1], device(-1, 0))]
     for key in near:
         pairs[key].wait_recv()
     fill(near)
     ahead(near, 0)
-    ahead(near, 1, 0, tokens // 2)
     take(-1, -1, (0, 1))
     take(1, 1, (0, -1))
     take(-1, 1)
     take(1, -1)
-    take(0, 2)
     u0 = [send("rs", part.at[up, hi], rx0.at[0], device(1, 0)),
           send("rs", part.at[um, lo], rx0.at[1], device(-1, 0))]
-    ahead(near, 1, tokens // 2)
+    ahead(near, 1)
     take(2, 1, (0, -1))
     take(2, -1)
-    mids = [(2, 0), (0, 2), (-1, -1), (1, 1), (-1, 1), (1, -1)]
+    mids = [(-1, -1), (1, 1), (-1, 1), (1, -1)]
     for copy in u1:
         copy.wait_recv()
     half = side // 2
@@ -229,11 +228,10 @@
     for key in mids:
         pairs[key].wait_recv()
     fill(mids)
-    ahead(mids, 0, 0, tokens * 3 // 4)
+    ahead(mids, 0)
     take(-1, 2)
     take(1, 2)
     take(2, 2)
-    ahead(mids, 0, tokens * 3 // 4)
     ahead(mids, 1)
 
     far = [(2, 1), (2, -1), (-1, 2), (1, 2), (2, 2)]
@@ -243,10 +241,6 @@
         copy.wait_recv()
     q[:half] = (part[u, :half].astype(F32) + rx2[0].astype(F32) + rx0[1].astype(F32)).astype(BF16)
     q[half:] = (part[u, half:].astype(F32) + rx2[1].astype(F32) + rx0[0].astype(F32)).astype(BF16)
-
-    @pl.when(rank_of(peers[5][0]) > rank)
-    def _():
-        pl.semaphore_wait(ready.at[5], 1)
 
     vs = [send("rs", q.at[(v + d) % side], ry.at[d - 1], device(0, d)) for d in (2, 1, 3)]
     fill(far)

time: 38.5 us -> 38.3 us (level); the launches traced: 38.4 us -> 37.7 us
  Pallas kernels: 37.6 us -> 36.9 us
    pallas_call x1, Pallas kernels: 33.6 us -> 32.9 us  [local_step(): pl.pallas_call(body, in_specs=[hbm] * 6, out_specs=[vmem] * len(outs), ou...]
where the time goes in v7:
time: 38.3 us; the launch traced here: 37.7 us
  Pallas kernels  36.9 us (96%)
  between operations  0.8 us (2%)
    pallas_call x1, Pallas kernels, local_step(): pl.pallas_call(body, in_specs=[hbm] * 6, out_specs=[vmem] * len(outs), ou...  32.9 us
    pallas_call x1, Pallas kernels, local_step(): pl.pallas_call(second, in_specs=[vmem] * len(parts), out_specs=[hbm] * 3,...  3.98 us

profile of v7, /device:TPU:1, one launch (start us, length us, event | category | flops | bytes accessed | tf_op | source)
XLA Modules:
  0.0 37.7 jit_solution(5876783490319408816)
XLA Ops:
  0.6 32.9 %mlp_step.1 = (bf16[288,2048]{1,0:T(8,128)(2,1)S(1)}, bf16[288,2048]{1,0:T(8,128)(2,1)S(1)}, f32[3,288,768]{2,1,0:T(8,128)S(1)}, f32[3,24,288]{2,1,0:T(8,128)S(1...) custom-call(bf16[2,288,2048]{2,1,0:T(8,128)(2,1)} %bitcast.9, ...), custom_call_target="tpu_custom_call" | custom-call | tf_op jit(solution)/shard_map/mlp_step/pallas_call | solution.py:320
  33.5 4.0 %second.1 = (bf16[2,288,2048]{2,1,0:T(8,128)(2,1)}, f32[3,24,288]{2,1,0:T(8,128)}, f32[3,288,768]{2,1,0:T(8,128)}) custom-call(bf16[288,2048]{1,0:T(8,128)(2,1)S(1)} %get-tuple-element.15.dx0, bf16[288,2048]{1,0:T(8,128)(2,1)S(1)} %get-tuple-element.16.dx1, f32[3,288,768]{2,1,0:T(8,128)S(1)} %get-tuple-element.17.acc, ...), custom_call_target="tpu_custom_call" | custom-call | tf_op jit(solution)/shard_map/second/pallas_call | solution.py:359
